TPU v7x, 16 devices: a whole 2x2x2 slice. The times are simulated.
16 devices in a mesh: dp: 4 (over z, y), tp: 4 (over x, core).
Axes of the slice: x: 2, y: 2, z: 2, core: 2. Of those that a mesh axis runs over, the one named last changes fastest.
Arguments:
- hidden: bfloat16 [128, 512, 768], P('dp')
- positions: int32 [128, 80], P('dp')
- labels: int32 [128, 80], P('dp')
- weights: float32 [128, 80], P('dp')
- w_t: bfloat16 [768, 768], replicated
- b_t: float32 [768], replicated
- gamma: float32 [768], replicated
- beta: float32 [768], replicated
- embed: bfloat16 [50304, 768], P('tp')
- out_bias: float32 [50304], P('tp')
Outputs:
- output 1: float32 [], replicated
- output 2: bfloat16 [128, 512, 768], P('dp')
- output 3: float32 [768, 768], replicated
- output 4: float32 [768], replicated
- output 5: float32 [768], replicated
- output 6: float32 [768], replicated
- output 7: float32 [50304, 768], P('tp')
- output 8: float32 [50304], P('tp')
All inputs are finite; a program needn't handle non-finite values.
Results may differ from a plain program's by a relative error of at most 0.001.
Values sent between devices are 32-bit elements.
A program may use at most 1 GiB of HBM per device.

v0:
```python
import jax
import jax.numpy as jnp
from jax import lax
from jax.sharding import PartitionSpec as P

LN_EPS = 1e-12
LOSS_EPS = 1e-5


def gelu_norm(pre_act, gamma, beta):
    activated = jax.nn.gelu(pre_act, approximate=False)
    mean_val = jnp.mean(activated, axis=-1, keepdims=True)
    centered = activated - mean_val
    variance = jnp.mean(centered * centered, axis=-1, keepdims=True)
    return centered * lax.rsqrt(variance + LN_EPS) * gamma + beta


def solution(mesh):
    def local_step(hidden, positions, labels, weights, w_t, b_t, gamma, beta, embed, out_bias):
        batch, seq_len, width = hidden.shape
        max_pred = positions.shape[1]
        shard_vocab = embed.shape[0]
        pos_hot = (positions[:, :, None] == jnp.arange(seq_len, dtype=jnp.int32)[None, None, :]).astype(jnp.bfloat16)
        picked = jnp.einsum("bps,bsd->bpd", pos_hot, hidden, preferred_element_type=jnp.float32).astype(jnp.bfloat16)
        tok_rows = picked.reshape(batch * max_pred, width)
        pre_act = jnp.dot(tok_rows, w_t, preferred_element_type=jnp.float32) + b_t
        normed, norm_vjp = jax.vjp(gelu_norm, pre_act, gamma, beta)
        t_bf = normed.astype(jnp.bfloat16)
        logits = jnp.einsum("nd,vd->nv", t_bf, embed, preferred_element_type=jnp.float32) + out_bias
        row_max = lax.pmax(jnp.max(logits, axis=1), "tp")
        shifted = jnp.exp(logits - row_max[:, None])
        sum_exp = lax.psum(jnp.sum(shifted, axis=1), "tp")
        local_lab = labels.reshape(-1) - lax.axis_index("tp") * shard_vocab
        lab_hot = local_lab[:, None] == jnp.arange(shard_vocab, dtype=jnp.int32)[None, :]
        target_logit = lax.psum(jnp.sum(jnp.where(lab_hot, logits, 0.0), axis=1), "tp")
        flat_w = weights.reshape(-1)
        denom = lax.psum(jnp.sum(flat_w), "dp") + LOSS_EPS
        log_norm = jnp.log(sum_exp) + row_max
        loss = lax.psum(jnp.sum(flat_w * (log_norm - target_logit)), "dp") / denom
        soft_probs = shifted * (1.0 / sum_exp)[:, None]
        d_logits = jnp.where(lab_hot, soft_probs - 1.0, soft_probs) * (flat_w / denom)[:, None]
        dz_bf = d_logits.astype(jnp.bfloat16)
        d_embed = lax.psum(jnp.einsum("nv,nd->vd", dz_bf, t_bf, preferred_element_type=jnp.float32), "dp")
        d_out_bias = lax.psum(jnp.sum(d_logits, axis=0), "dp")
        d_normed = lax.psum(jnp.einsum("nv,vd->nd", dz_bf, embed, preferred_element_type=jnp.float32), "tp")
        d_pre, d_gamma, d_beta = norm_vjp(d_normed)
        d_pre_bf = d_pre.astype(jnp.bfloat16)
        d_w_t = lax.psum(jnp.einsum("nd,ne->de", tok_rows, d_pre_bf, preferred_element_type=jnp.float32), "dp")
        d_b_t = lax.psum(jnp.sum(d_pre, axis=0), "dp")
        d_gamma = lax.psum(d_gamma, "dp")
        d_beta = lax.psum(d_beta, "dp")
        d_rows = jnp.einsum("ne,de->nd", d_pre_bf, w_t, preferred_element_type=jnp.float32).astype(jnp.bfloat16)
        d_hidden = jnp.einsum("bps,bpd->bsd", pos_hot, d_rows.reshape(batch, max_pred, width), preferred_element_type=jnp.float32).astype(jnp.bfloat16)
        return loss, d_hidden, d_w_t, d_b_t, d_gamma, d_beta, d_embed, d_out_bias

    in_specs = (P("dp", None, None), P("dp", None), P("dp", None), P("dp", None), P(None, None), P(None), P(None), P(None), P("tp", None), P("tp"))
    out_specs = (P(), P("dp", None, None), P(None, None), P(None), P(None), P(None), P("tp", None), P("tp"))
    return jax.shard_map(local_step, mesh=mesh, in_specs=in_specs, out_specs=out_specs, check_vma=False)
```

profile of v0, /device:TPU:0, one launch (start us, length us, event | category | flops | bytes accessed | tf_op | source)
XLA Modules:
  0.0 1247.1 jit_solution(5714578093456478155)
XLA Ops:
  7.2 1.5 reshape.75
  8.7 1.3 reduce_sum.129
  10.0 12.3 psum.80
  22.4 0.7 broadcast_subtract_fusion
  23.1 0.7 sub.42
  23.8 10.5 fusion.14
  34.3 25.7 %fusion.23 = (f32[2560]{0:T(1024)S(1)}, f32[2560,768]{0,1:T(8,128)S(1)}, f32[2560,768]{0,1:T(8,128)}, f32[2560,768]{0,1:T(8,128)}) fusion(f32[768]{0:T(1024)S(1)} %copy-done.25, bf16[2560,768]{1,0:T(8,128)(2,1)S(1)} %bitcast.19, bf16[768,768]{1,0:T(8,128)(2,1)S(1)} %copy-done), kind=kOutput, calls=%fused_computation.55 | convolution fusion | flops 3149657600 | bytes 28718080 | tf_op jit(solution)/shard_map/dot_general | solution.py:26
  60.1 3.1 copy-done.1
  63.1 0.9 multiply_reduce_fusion.2
  64.6 66.3 %add_reduce_fusion = (f32[2560]{0:T(1024)S(1)}, f32[2560,12576]{0,1:T(8,128)}) fusion(f32[12576]{0:T(1024)S(1)} %copy-done.9, bf16[12576,768]{1,0:T(8,128)(2,1)} %param.18, f32[2560,768]{0,1:T(8,128)} %copy-done.1, f32[768]{0:T(1024)S(1)} %copy-done.27, f32[768]{0:T(1024)S(1)} %copy-done.23, f32[2560]{0:T(1024)S(1)} %fusion.18, ...), kind=kOutput, calls=%fused_computation.6 | convolution fusion | flops 49525059584 | bytes 156046464 | tf_op jit(solution)/shard_map/nd,vd->nv/dot_general | solution.py:29
  130.9 10.1 pmax.7
  141.1 39.4 %fusion.1 = f32[2560]{0:T(1024)S(1)} fusion(f32[2560,12576]{0,1:T(8,128)} %get-tuple-element.29, f32[2560]{0:T(1024)S(1)} %pmax.7, f32[12576]{0:T(1024)S(1)} %copy-done.9), kind=kLoop, calls=%fused_computation.5 | loop fusion | flops 96581120 | bytes 128849024 | tf_op jit(solution)/shard_map/reduce_sum | solution.py:32
  180.5 10.1 psum.77
  191.3 91.1 %fusion.2 = (f32[12576]{0:T(1024)}, f32[2560]{0:T(1024)}, bf16[2560,12576]{0,1:T(8,128)(2,1)}) fusion(f32[2560,12576]{0,1:T(8,128)} %get-tuple-element.29, f32[2560]{0:T(1024)S(1)} %broadcast_divide_fusion, f32[2560]{0:T(1024)S(1)} %broadcast_divide_fusion.1, s32[2560]{0:T(1024)S(1)} %copy-done.21, f32[2560]{0:T(1024)S(1)} %pmax.7, f32[12576]{0:T(1024)S(1)} %copy-done.9), kind=kLoop, calls=%fused_computation.7 | loop fusion | flops 354125024 | bytes 193319168 | tf_op jit(solution)/shard_map/reduce_sum | solution.py:44
  282.5 61.3 %fusion.25 = f32[2560,768]{0,1:T(8,128)} fusion(bf16[2560,12576]{0,1:T(8,128)(2,1)} %get-tuple-element.26, bf16[12576,768]{1,0:T(8,128)(2,1)} %param.18), kind=kOutput, calls=%fused_computation.56 | convolution fusion | flops 49450844160 | bytes 91570176 | tf_op jit(solution)/shard_map/nv,vd->nd/dot_general | solution.py:45
  343.9 0.6 copy-done.7
  344.5 62.0 %fusion.19 = f32[12576,768]{1,0:T(8,128)} fusion(bf16[2560,12576]{0,1:T(8,128)(2,1)} %get-tuple-element.26, f32[2560,768]{0,1:T(8,128)} %copy-done.1, f32[768]{0:T(1024)S(1)} %copy-done.28, f32[768]{0:T(1024)S(1)} %copy-done.24, f32[2560]{0:T(1024)S(1)} %copy-done.14, f32[2560]{0:T(1024)S(1)} %copy-done.7), kind=kOutput, calls=%fused_computation.51 | convolution fusion | flops 49460674560 | bytes 110913536 | tf_op jit(solution)/shard_map/nv,nd->vd/dot_general | solution.py:43
  406.5 77.8 %all-reduce.5.cloned.1.call-done = f32[2560,768]{0,1:T(8,128)} async-done(((f32[2560,768]{0,1:T(8,128)}), f32[2560,768]{0,1:T(8,128)}) %all-reduce.5.cloned.1.call-update) | async-done | bytes 7864336 | tf_op jit(solution)/shard_map/psum | solution.py:45
  484.3 7.1 fusion.21
  492.1 2.2 copy-done.3
  494.3 3.5 multiply_reduce_fusion
  497.8 10.5 fusion.22
  508.4 6.8 fusion.15
  515.2 0.7 copy-done.22
  515.8 10.7 psum.78
  526.5 0.6 multiply_reduce_fusion.3
  527.2 21.3 %all-reduce = (f32[]{:T(128)}, f32[768]{0:T(1024)}, f32[768]{0:T(1024)}, f32[768]{0:T(1024)}, f32[12576]{0:T(1024)}) all-reduce(f32[]{:T(128)} %multiply_reduce_fusion.3, f32[768]{0:T(1024)S(1)} %get-tuple-element.21, f32[768]{0:T(1024)S(1)} %get-tuple-element.10, ...), channel_id=1, replica_groups=mesh['dp'=4,'tp'=4] {'dp'}, use_global_device_ids=true, to_apply=%region_9.10 | all-reduce | flops 14881 | bytes 119048 | tf_op jit(solution)/shard_map/psum | solution.py:39
  549.1 7.3 convolution_convert_fusion.1
  556.5 14.6 %convolution_convert_fusion = bf16[32,512,768]{2,1,0:T(8,128)(2,1)} fusion(bf16[32,80,768]{2,1,0:T(8,128)(2,1)} %bitcast.16, s32[32,80]{1,0:T(8,128)S(1)} %copy-done.8), kind=kOutput, calls=%fused_computation.9 | convolution fusion | flops 2027159552 | bytes 29108224 | tf_op jit(solution)/shard_map/bps,bpd->bsd/dot_general | solution.py:53
  571.1 637.0 %all-reduce.7.cloned.1.call-done = (f32[768,768]{1,0:T(8,128)}, f32[12576,768]{1,0:T(8,128)}) async-done(((f32[768,768]{1,0:T(8,128)}, f32[12576,768]{1,0:T(8,128)}), (f32[768,768]{1,0:T(8,128)}, f32[12576,768]{1,0:T(8,128)})) %all-reduce.7.cloned.1.call-update) | async-done | bytes 40992784 | tf_op jit(solution)/shard_map/psum | solution.py:48
  1208.1 3.2 copy.23
  1211.3 27.3 %copy.24 = f32[12576,768]{1,0:T(8,128)} copy(f32[12576,768]{1,0:T(8,128)} %get-tuple-element.38) | data formatting | bytes 77266944
  (69 shorter events, 1.5 us)
Async XLA Ops:
  7.2 27.2 %copy-start = (bf16[768,768]{1,0:T(8,128)(2,1)S(1)}, bf16[768,768]{1,0:T(8,128)(2,1)}, u32[]{:S(2)}) copy-start(bf16[768,768]{1,0:T(8,128)(2,1)} %param.14) | copy-start | bytes 3538948
  7.2 477.1 %all-reduce.5.cloned.1.call-start = ((), (), s32[]{:S(2)}) async-start(), calls=%async_computation | async-start | bytes 15728640 | tf_op jit(solution)/shard_map/psum | solution.py:45
  23.8 10.6 copy-start.25
  34.3 25.7 %copy-start.4 = (bf16[32,80,768]{2,1,0:T(8,128)(2,1)}, bf16[32,80,768]{2,1,0:T(8,128)(2,1)S(1)}, u32[]{:S(2)}) copy-start(bf16[32,80,768]{2,1,0:T(8,128)(2,1)S(1)} %fusion.14) | copy-start | bytes 11796484
  60.0 3.1 copy-start.1
  60.0 4.6 copy-start.9
  60.0 4.6 copy-start.23
  60.0 4.6 copy-start.27
  60.1 70.9 %copy-start.6 = (f32[2560]{0:T(1024)}, f32[2560]{0:T(1024)S(1)}, u32[]{:S(2)}) copy-start(f32[2560]{0:T(1024)S(1)} %broadcast_multiply_fusion) | copy-start | bytes 30724
  64.6 66.3 %copy-start.13 = (f32[2560]{0:T(1024)}, f32[2560]{0:T(1024)S(1)}, u32[]{:S(2)}) copy-start(f32[2560]{0:T(1024)S(1)} %fusion.18) | copy-start | bytes 30724
  141.1 50.3 %copy-start.11 = (f32[2560]{0:T(1024)}, f32[2560]{0:T(1024)S(1)}, u32[]{:S(2)}) copy-start(f32[2560]{0:T(1024)S(1)} %pmax.7) | copy-start | bytes 30724
  141.1 50.2 %copy-start.17 = (f32[2560]{0:T(1024)S(1)}, f32[2560]{0:T(1024)}, u32[]{:S(2)}) copy-start(f32[2560]{0:T(1024)} %reshape.75) | copy-start | bytes 30724
  141.1 50.3 %copy-start.21 = (s32[2560]{0:T(1024)S(1)}, s32[2560]{0:T(1024)}, u32[]{:S(2)}) copy-start(s32[2560]{0:T(1024)} %sub.42) | copy-start | bytes 30724
  190.6 91.8 %copy-start.19 = (f32[2560]{0:T(1024)}, f32[2560]{0:T(1024)S(1)}, u32[]{:S(2)}) copy-start(f32[2560]{0:T(1024)S(1)} %psum.77) | copy-start | bytes 30724
  343.8 0.7 copy-start.7
  343.8 0.7 copy-start.14
  343.8 0.7 copy-start.24
  343.8 0.7 copy-start.28
  343.8 864.3 %all-reduce.7.cloned.1.call-start = ((), (), s32[]{:S(2)}) async-start(), calls=%async_computation.1 | async-start | bytes 81985536 | tf_op jit(solution)/shard_map/psum | solution.py:48
  406.5 85.0 %copy-start.16 = (f32[2560]{0:T(1024)S(1)}, f32[2560]{0:T(1024)}, u32[]{:S(2)}) copy-start(f32[2560]{0:T(1024)} %copy-done.15) | copy-start | bytes 30724
  484.3 7.8 copy-start.2
  484.3 10.0 copy-start.3
  484.3 13.5 %slice-start = ((s8[7864320]{0:T(1024)(128)(4,1)}), s8[4194304]{0:T(1024)(128)(4,1)S(1)}, s32[]{:S(2)}) async-start(s8[7864320]{0:T(1024)(128)(4,1)} %bitcast.17), calls=%async_computation.2 | async-start | bytes 8388608
  494.3 3.5 slice-start.1
  494.3 3.5 copy-start.26
  497.8 10.5 copy-start.5
  515.1 0.7 copy-start.22
  515.1 11.4 copy-start.12
  515.1 11.4 copy-start.18
  515.1 11.4 copy-start.20
  515.1 12.0 copy-start.10
  549.1 7.3 copy-start.8
  (1 other events, 0.6 us)
Sparse Core Ops, SparseCore 0:
  343.9 140.3 all-reduce.4
  515.3 692.7 all-reduce.6
where the time goes:
time: 1250 us
  waiting for transfers between devices  715 us (57%)
  matrix products  254 us (20%)
  other arithmetic  155 us (12%)
  blocking collectives  64.6 us (5%)
  local copies, waits for them, and re-layouts  40.6 us (3%)
  between operations  17.3 us (1%)
    psum x1, waiting for transfers between devices, local_step(): lax.psum(jnp.einsum('nd,ne->de', tok_rows, d_pre_bf, preferred_element_ty...  637 us
    reduce_sum x1, other arithmetic, local_step(): d_out_bias = lax.psum(jnp.sum(d_logits, axis=0), 'dp')  91.1 us
    psum x1, waiting for transfers between devices, local_step(): lax.psum(jnp.einsum('nv,vd->nd', dz_bf, embed, preferred_element_type=jnp...  77.8 us
    dot_general x1, matrix products, local_step(): jnp.einsum('nd,vd->nv', t_bf, embed, preferred_element_type=jnp.float32)  66.3 us
    dot_general x1, matrix products, local_step(): jnp.einsum('nv,nd->vd', dz_bf, t_bf, preferred_element_type=jnp.float32)  62 us
    dot_general x1, matrix products, local_step(): jnp.einsum('nv,vd->nd', dz_bf, embed, preferred_element_type=jnp.float32)  61.3 us
    reduce_sum x1, other arithmetic, local_step(): sum_exp = lax.psum(jnp.sum(shifted, axis=1), 'tp')  39.4 us
    unnamed x64, local copies, waits for them, and re-layouts  38.4 us
  transfers between devices with their start and end apart: 2, of which 2 were waited for; matrix products, arithmetic and copies ran while one was open for 7% of the time, Pallas kernels for 0%

commit v1 on v0

v1 whole, which is shorter than its diff:
```python
import functools

import jax
import jax.numpy as jnp
from jax import lax
from jax.experimental import pallas as pl
from jax.experimental.pallas import tpu as pltpu
from jax.sharding import PartitionSpec as P

LN_EPS = 1e-12
LOSS_EPS = 1e-5
VOCAB_BLOCKS = 6
TOK = 256
CHUNK = 256
STAGES = 4
PICK = 96
OFF = 1e30
VMEM_LIMIT = 67_000_000


def gelu_norm(pre_act, gamma, beta):
    activated = jax.nn.gelu(pre_act, approximate=False)
    mean_val = jnp.mean(activated, axis=-1, keepdims=True)
    centered = activated - mean_val
    variance = jnp.mean(centered * centered, axis=-1, keepdims=True)
    return centered * lax.rsqrt(variance + LN_EPS) * gamma + beta


def dot_nt(a, b):
    return lax.dot_general(a, b, (((1,), (1,)), ((), ())), preferred_element_type=jnp.float32)


def dot_tn(a, b):
    return lax.dot_general(a, b, (((0,), (0,)), ((), ())), preferred_element_type=jnp.float32)


def dot_nn(a, b):
    return jnp.dot(a, b, preferred_element_type=jnp.float32)


def hot_rows(row, seq_len):
    ids = lax.broadcasted_iota(jnp.int32, (seq_len, PICK), 0)
    return jnp.where(ids == row[:, :PICK], 1.0, 0.0).astype(jnp.bfloat16)


def pick_kernel(base_ref, idx_ref, hidden_ref, out_ref, acc):
    seq = pl.program_id(0)

    @pl.when(seq == 0)
    def _():
        acc[...] = jnp.zeros_like(acc)

    rows = dot_tn(hot_rows(idx_ref[0], hidden_ref.shape[1]), hidden_ref[0])
    base = pl.multiple_of(base_ref[seq], 8)
    acc[pl.ds(base, 16), :] += rows[:16]
    acc[pl.ds(base + 16, PICK - 16), :] = rows[16:]

    @pl.when(seq == pl.num_programs(0) - 1)
    def _():
        out_ref[...] = acc[...].astype(jnp.bfloat16)


def place_kernel(base_ref, idx_ref, rows_ref, out_ref):
    seq = pl.program_id(0)
    base = pl.multiple_of(base_ref[seq], 8)
    rows = rows_ref[pl.ds(base, PICK), :].astype(jnp.bfloat16)
    out_ref[0] = dot_nn(hot_rows(idx_ref[0], out_ref.shape[1]), rows).astype(jnp.bfloat16)


def for_blocks(count, body):
    def pair(step, carry):
        body(2 * step, 0)
        body(2 * step + 1, 1)
        return carry

    lax.fori_loop(0, count // 2, pair, 0)

    @pl.when(count % 2 == 1)
    def _():
        body(count - 1, 0)


def tile_bias(bias_ref):
    bias = bias_ref[...]
    return jnp.concatenate([bias] * (TOK // bias.shape[1]), axis=1)


def stats_kernel(count_ref, lab_ref, tok_ref, embed_ref, bias_ref, out_ref, z0, z1):
    vblk = pl.program_id(0)
    height = embed_ref.shape[0]

    @pl.when(vblk == 0)
    def _():
        out_ref[...] = jnp.zeros_like(out_ref)
        out_ref[0:1, :] = jnp.full((1, out_ref.shape[1]), -jnp.inf, jnp.float32)

    def body(block, slot):
        z_ref = (z0, z1)[slot]
        cols = pl.ds(pl.multiple_of(block * TOK, TOK), TOK)
        z_ref[...] = dot_nt(embed_ref[...], tok_ref[cols, :]) + tile_bias(bias_ref)
        old_max = out_ref[0:1, cols]
        new_max = jnp.maximum(old_max, jnp.max(z_ref[...], axis=0, keepdims=True))
        part = jnp.sum(jnp.exp(z_ref[...] - new_max), axis=0, keepdims=True)
        ids = lax.broadcasted_iota(jnp.int32, (height, TOK), 0)
        hit = ids == lab_ref[0:1, cols] - vblk * height
        target = jnp.sum(jnp.where(hit, z_ref[...], 0.0), axis=0, keepdims=True)
        out_ref[1:2, cols] = out_ref[1:2, cols] * jnp.exp(old_max - new_max) + part
        out_ref[0:1, cols] = new_max
        out_ref[2:3, cols] += target

    for_blocks(count_ref[0], body)


def logit_grad(vblk, block, tok, lab_ref, meta_ref, embed_ref, bias_ref, dbias_ref, z_ref, dz_ref):
    cols = pl.ds(pl.multiple_of(block * TOK, TOK), TOK)
    height = embed_ref.shape[0]
    z_ref[...] = dot_nt(embed_ref[...], tok)
    ids = lax.broadcasted_iota(jnp.int32, (height, TOK), 0)
    hit = ids == lab_ref[0:1, cols] - vblk * height
    probs = jnp.exp(z_ref[...] + tile_bias(bias_ref) - meta_ref[0:1, cols]) * meta_ref[1:2, cols]
    dz = probs - jnp.where(hit, meta_ref[2:3, cols], 0.0)
    lanes = dbias_ref.shape[1]
    part = dz[:, :lanes]
    for k in range(1, TOK // lanes):
        part = part + dz[:, k * lanes:(k + 1) * lanes]
    dbias_ref[...] += part
    dz_ref[...] = dz.astype(jnp.bfloat16)


def own_kernel(count_ref, lab_ref, meta_ref, tok_ref, embed_ref, bias_ref, dembed_ref, dbias_ref, dtok_ref, z0, z1, dz0, dz1):
    vblk = pl.program_id(0)

    @pl.when(vblk == 0)
    def _():
        dtok_ref[...] = jnp.zeros_like(dtok_ref)

    dembed_ref[...] = jnp.zeros_like(dembed_ref)
    dbias_ref[...] = jnp.zeros_like(dbias_ref)

    def body(block, slot):
        z_ref, dz_ref = (z0, z1)[slot], (dz0, dz1)[slot]
        rows = pl.ds(pl.multiple_of(block * TOK, TOK), TOK)
        tok = tok_ref[rows, :]
        logit_grad(vblk, block, tok, lab_ref, meta_ref, embed_ref, bias_ref, dbias_ref, z_ref, dz_ref)
        dembed_ref[...] += dot_nn(dz_ref[...], tok)
        dtok_ref[rows, :] += dot_tn(dz_ref[...], embed_ref[...])

    for_blocks(count_ref[0], body)


def rest_kernel(plan_ref, src_ref, dst_ref, lab_ref, meta_ref, embed_ref, bias_ref, dembed_in_ref, tok_hbm, dembed_ref, dbias_ref, tok_ref, stage, sems, z0, z1, dz0, dz1):
    vblk = pl.program_id(0)
    chunks = plan_ref[1]

    def fetch(chunk):
        slot = lax.rem(chunk, STAGES)
        src = tok_hbm.at[pl.ds(pl.multiple_of(src_ref[chunk], CHUNK), CHUNK), :]
        return pltpu.make_async_copy(src, stage.at[slot], sems.at[slot])

    @pl.when(vblk == 0)
    def _():
        end = pl.multiple_of(plan_ref[2], 16)
        tok_ref[pl.ds(end, TOK), :] = jnp.zeros((TOK, tok_ref.shape[1]), jnp.bfloat16)
        for first in range(STAGES):
            @pl.when(first < chunks)
            def _():
                fetch(first).start()

        def take(chunk, carry):
            fetch(chunk).wait()
            dst = pl.multiple_of(dst_ref[chunk], 16)
            tok_ref[pl.ds(dst, CHUNK), :] = stage[lax.rem(chunk, STAGES)].astype(jnp.bfloat16)

            @pl.when(chunk + STAGES < chunks)
            def _():
                fetch(chunk + STAGES).start()
            return carry

        lax.fori_loop(0, chunks, take, 0)

    dembed_ref[...] = dembed_in_ref[...]
    dbias_ref[...] = jnp.zeros_like(dbias_ref)

    def body(block, slot):
        z_ref, dz_ref = (z0, z1)[slot], (dz0, dz1)[slot]
        tok = tok_ref[pl.ds(pl.multiple_of(block * TOK, TOK), TOK), :]
        logit_grad(vblk, block, tok, lab_ref, meta_ref, embed_ref, bias_ref, dbias_ref, z_ref, dz_ref)
        dembed_ref[...] += dot_nn(dz_ref[...], tok)

    for_blocks(plan_ref[0], body)


def whole(shape):
    return pl.BlockSpec(shape, lambda *_: (0,) * len(shape))


def by_rows(shape):
    return pl.BlockSpec(shape, lambda step, *_: (step,) + (0,) * (len(shape) - 1))


def run(kernel, scalars, grid, args, in_specs, out_specs, out_shape, scratch, flops, aliases=None):
    return pl.pallas_call(
        kernel,
        grid_spec=pltpu.PrefetchScalarGridSpec(
            num_scalar_prefetch=len(scalars), grid=(grid,), in_specs=in_specs, out_specs=out_specs, scratch_shapes=scratch
        ),
        out_shape=out_shape,
        input_output_aliases=aliases or {},
        compiler_params=pltpu.CompilerParams(dimension_semantics=("arbitrary",), vmem_limit_bytes=VMEM_LIMIT),
        cost_estimate=pl.CostEstimate(flops=flops, bytes_accessed=40_000_000, transcendentals=0),
    )(*scalars, *args)


def solution(mesh):
    groups, shards = mesh.shape["dp"], mesh.shape["tp"]
    f32, bf16, i32 = jnp.float32, jnp.bfloat16, jnp.int32

    def local_step(hidden, positions, labels, weights, w_t, b_t, gamma, beta, embed, out_bias):
        batch, seq_len, width = hidden.shape
        max_pred = positions.shape[1]
        rows = batch * max_pred
        vocab = embed.shape[0]
        height = vocab // VOCAB_BLOCKS
        me_dp, me_tp = lax.axis_index("dp"), lax.axis_index("tp")

        live = jnp.sum(weights, axis=1).astype(i32)
        seqs = jnp.arange(batch, dtype=i32)
        offset = jnp.sum(jnp.where(seqs[None, :] < seqs[:, None], live[None, :], 0), axis=1)
        base = jnp.minimum(offset // 8 * 8, rows - PICK)
        slots = jnp.arange(max_pred, dtype=i32)
        alive = slots[None, :] < live[:, None]
        place = jnp.where(alive, slots[None, :] + (offset - base)[:, None], -1)
        lanes = jnp.arange(128, dtype=i32)
        idx_rows = jnp.sum(jnp.where(place[:, None, :] == lanes[None, :, None], positions[:, None, :] + 1, 0), axis=2) - 1
        idx_rows = idx_rows.reshape(batch, 1, 128)
        packed = jnp.where(alive, slots[None, :] + offset[:, None], -1).reshape(-1)
        lab = jnp.sum(jnp.where(packed[None, :] == jnp.arange(rows, dtype=i32)[:, None], labels.reshape(-1)[None, :] + 1, 0), axis=1) - 1
        count = jnp.sum(live)
        blocks = ((count + TOK - 1) // TOK).reshape(1)

        picked = run(
            pick_kernel, (base,), batch, (idx_rows, hidden),
            [by_rows((1, 1, 128)), by_rows((1, seq_len, width))], whole((rows, width)),
            jax.ShapeDtypeStruct((rows, width), bf16), [pltpu.VMEM((rows, width), f32)], 8_000_000_000,
        )
        pre_act = jnp.dot(picked, w_t, preferred_element_type=f32) + b_t
        normed, norm_vjp = jax.vjp(gelu_norm, pre_act, gamma, beta)
        tok = normed.astype(bf16)
        share = rows // shards
        mine = lax.dynamic_slice(normed, (me_tp * share, 0), (share, width))
        tok_all = lax.all_gather(mine, ("dp", "tp"), tiled=True)

        bias = jnp.broadcast_to(out_bias[:, None], (vocab, 128))
        local_lab = jnp.where(lab >= 0, lab - me_tp * vocab, -1)
        z_scratch = [pltpu.VMEM((height, TOK), f32)] * 2
        dz_scratch = [pltpu.VMEM((height, TOK), bf16)] * 2
        stats = run(
            stats_kernel, (blocks,), VOCAB_BLOCKS, (local_lab[None, :], tok, embed, bias),
            [whole((1, rows)), whole((rows, width)), by_rows((height, width)), by_rows((height, 128))], whole((8, rows)),
            jax.ShapeDtypeStruct((8, rows), f32), z_scratch, 25_000_000_000,
        )
        packet = jnp.concatenate([stats[:3], lab.astype(f32)[None, :]], axis=0)
        packets = lax.all_gather(packet, ("dp", "tp")).reshape(groups, shards, 4, rows)
        labs = packets[:, 0, 3, :].astype(i32)
        valid = labs >= 0
        maxes = jnp.where(valid[:, None, :], packets[:, :, 0, :], 0.0)
        row_max = jnp.max(maxes, axis=1)
        sum_exp = jnp.where(valid, jnp.sum(packets[:, :, 1, :] * jnp.exp(maxes - row_max[:, None, :]), axis=1), 1.0)
        target = jnp.sum(packets[:, :, 2, :], axis=1)
        lives = jnp.sum(valid, axis=1).astype(i32)
        denom = jnp.sum(lives).astype(f32) + LOSS_EPS
        loss = jnp.sum(jnp.where(valid, jnp.log(sum_exp) + row_max - target, 0.0)) / denom
        inv = 1.0 / denom
        metas = jnp.stack([
            jnp.where(valid, row_max, OFF),
            jnp.where(valid, (1.0 / sum_exp) * inv, 0.0),
            jnp.where(valid, inv, 0.0),
            jnp.where(valid, labs - me_tp * vocab, -1).astype(f32),
        ], axis=1)

        own_meta = lax.dynamic_index_in_dim(metas, me_dp, 0, keepdims=False)
        d_embed, d_bias_own, d_tok = run(
            own_kernel, (blocks,), VOCAB_BLOCKS, (local_lab[None, :], own_meta, tok, embed, bias),
            [whole((1, rows)), whole((4, rows)), whole((rows, width)), by_rows((height, width)), by_rows((height, 128))],
            [by_rows((height, width)), by_rows((height, 128)), whole((rows, width))],
            [jax.ShapeDtypeStruct((vocab, width), f32), jax.ShapeDtypeStruct((vocab, 128), f32), jax.ShapeDtypeStruct((rows, width), f32)],
            z_scratch + dz_scratch, 75_000_000_000,
        )
        d_normed = lax.psum(d_tok, "tp")

        cap = (groups - 1) * rows
        meta = jnp.concatenate([jnp.full((1, cap + TOK), OFF, f32), jnp.zeros((2, cap + TOK), f32), jnp.full((1, cap + TOK), -1.0, f32)], axis=0)
        pos = jnp.int32(0)
        ids = jnp.arange(cap // CHUNK, dtype=i32)
        src, dst, chunks = jnp.zeros_like(ids), jnp.zeros_like(ids), jnp.int32(0)
        for k in range(1, groups):
            peer = lax.rem(me_dp + k, groups)
            meta = lax.dynamic_update_slice(meta, lax.dynamic_index_in_dim(metas, peer, 0, keepdims=False), (0, pos))
            size = lax.dynamic_index_in_dim(lives, peer, 0, keepdims=False)
            parts = (size + CHUNK - 1) // CHUNK
            inside = ids >= chunks
            src = jnp.where(inside, peer * rows + (ids - chunks) * CHUNK, src)
            dst = jnp.where(inside, pos + (ids - chunks) * CHUNK, dst)
            chunks = chunks + parts
            last = pos + parts * CHUNK
            pos = pos + (size + 15) // 16 * 16
        plan = jnp.stack([(pos + TOK - 1) // TOK, chunks, last])
        meta_lab = meta[3:4].astype(i32)
        d_embed, d_bias_rest = run(
            rest_kernel, (plan, src, dst), VOCAB_BLOCKS, (meta_lab, meta, embed, bias, d_embed, tok_all),
            [whole((1, cap + TOK)), whole((4, cap + TOK)), by_rows((height, width)), by_rows((height, 128)), by_rows((height, width)), pl.BlockSpec(memory_space=pl.ANY)],
            [by_rows((height, width)), by_rows((height, 128))],
            [jax.ShapeDtypeStruct((vocab, width), f32), jax.ShapeDtypeStruct((vocab, 128), f32)],
            [pltpu.VMEM((cap + TOK, width), bf16), pltpu.VMEM((STAGES, CHUNK, width), f32), pltpu.SemaphoreType.DMA((STAGES,))] + z_scratch + dz_scratch,
            150_000_000_000, {7: 0},
        )
        d_out_bias = jnp.sum(d_bias_own + d_bias_rest, axis=1)

        d_pre, d_gamma, d_beta = norm_vjp(d_normed)
        d_pre_bf = d_pre.astype(bf16)
        d_w_t = jnp.einsum("nd,ne->de", picked, d_pre_bf, preferred_element_type=f32)
        d_b_t = jnp.sum(d_pre, axis=0)
        d_w_t, d_b_t, d_gamma, d_beta = lax.psum((d_w_t, d_b_t, d_gamma, d_beta), "dp")
        d_rows = jnp.einsum("ne,de->nd", d_pre_bf, w_t, preferred_element_type=f32)
        d_hidden = run(
            place_kernel, (base,), batch, (idx_rows, d_rows),
            [by_rows((1, 1, 128)), whole((rows, width))], by_rows((1, seq_len, width)),
            jax.ShapeDtypeStruct((batch, seq_len, width), bf16), [], 8_000_000_000,
        )
        return loss, d_hidden, d_w_t, d_b_t, d_gamma, d_beta, d_embed, d_out_bias

    in_specs = (P("dp", None, None), P("dp", None), P("dp", None), P("dp", None), P(None, None), P(None), P(None), P(None), P("tp", None), P("tp"))
    out_specs = (P(), P("dp", None, None), P(None, None), P(None), P(None), P(None), P("tp", None), P("tp"))
    return jax.shard_map(local_step, mesh=mesh, in_specs=in_specs, out_specs=out_specs, check_vma=False)
```

time: 1250 us -> 932 us (0.75)
  Pallas kernels: 0 us -> 510 us
  waiting for transfers between devices: 715 us -> 231 us
  matrix products: 254 us -> 38.2 us
  other arithmetic: 155 us -> 50.8 us
  blocking collectives: 64.6 us -> 42 us
  local copies, waits for them, and re-layouts: 40.6 us -> 25.7 us
    pallas_call x0 -> x5, Pallas kernels: none -> 510 us  [run(): pl.pallas_call(kernel, grid_spec=pltpu.PrefetchScalarGridSpec(num_scalar_...]
    psum x2, waiting for transfers between devices: 715 us -> 231 us  [the longest x1 231 us: local_step(): d_normed = lax.psum(d_tok, 'tp')]
    dot_general x8 -> x3, matrix products: 254 us -> 38.2 us  [the longest x1 23.5 us: local_step(): pre_act = jnp.dot(picked, w_t, preferred_element_type=f32) + b_t]
    reduce_sum x5 -> x9, other arithmetic: 143 us -> 20.9 us  [the longest x1 8.02 us: local_step(): d_b_t = jnp.sum(d_pre, axis=0)]
    psum x4 -> x1, blocking collectives: 54.5 us -> 17.4 us  [local_step(): lax.psum((d_w_t, d_b_t, d_gamma, d_beta), 'dp')]
    unnamed x64 -> x62, local copies, waits for them, and re-layouts: 38.4 us -> 10.8 us
    all_gather x0 -> x1, blocking collectives: none -> 24.6 us  [local_step(): lax.all_gather(packet, ('dp', 'tp')).reshape(groups, shards, 4, rows)]
  transfers between devices with their start and end apart: 2 -> 3, of which waited for: 2 -> 1; matrix products, arithmetic and copies ran while one was open for 7% -> 6% of each run, Pallas kernels for 0% -> 33%
where the time goes in v1:
time: 932 us; the launch traced here: 922 us
  Pallas kernels  510 us (55%)
  waiting for transfers between devices  231 us (25%)
  other arithmetic  50.8 us (5%)
  blocking collectives  42 us (5%)
  matrix products  38.2 us (4%)
  local copies, waits for them, and re-layouts  25.7 us (3%)
  between operations  23.7 us (3%)
    pallas_call x5, Pallas kernels, run(): pl.pallas_call(kernel, grid_spec=pltpu.PrefetchScalarGridSpec(num_scalar_...  510 us
    psum x1, waiting for transfers between devices, local_step(): d_normed = lax.psum(d_tok, 'tp')  231 us
    all_gather x1, blocking collectives, local_step(): lax.all_gather(packet, ('dp', 'tp')).reshape(groups, shards, 4, rows)  24.6 us
    dot_general x1, matrix products, local_step(): pre_act = jnp.dot(picked, w_t, preferred_element_type=f32) + b_t  23.5 us
  transfers between devices with their start and end apart: 3, of which 1 were waited for; matrix products, arithmetic and copies ran while one was open for 6% of the time, Pallas kernels for 33%

profile of v1, /device:TPU:0, one launch (start us, length us, event | category | flops | bytes accessed | tf_op | source)
XLA Modules:
  0.0 921.6 jit_solution(7778408498148069062)
XLA Ops:
  8.1 0.8 reduce_sum.180
  9.0 1.2 fusion.24
  12.4 1.0 select_reduce_fusion.1
  14.1 2.9 select_reduce_fusion
  17.6 27.9 %shard_map.161 = bf16[2560,768]{1,0:T(8,128)(2,1)} custom-call(s32[32]{0:T(128)} %get-tuple-element.36.base_ref, s32[32,1,128]{2,1,0:T(1,128)} %bitcast.81, bf16[32,512,768]{2,1,0:T(8,128)(2,1)} %hidden_ref.1), custom_call_target="tpu_custom_call" | custom-call | flops 8000000000 | bytes 40000000 | tf_op jit(solution)/shard_map/pallas_call | solution.py:202
  45.6 23.5 %fusion.22 = (f32[2560]{0:T(1024)S(1)}, f32[2560,768]{1,0:T(8,128)S(1)}, f32[2560,768]{1,0:T(8,128)}, f32[2560,768]{1,0:T(8,128)}) fusion(f32[768]{0:T(1024)S(1)} %copy-done.24, bf16[2560,768]{1,0:T(8,128)(2,1)} %shard_map.161, bf16[768,768]{1,0:T(8,128)(2,1)} %param.14), kind=kOutput, calls=%fused_computation.91 | convolution fusion | flops 3149657600 | bytes 28718080 | tf_op jit(solution)/shard_map/dot_general | solution.py:246
  69.1 3.1 copy-done
  72.2 1.8 multiply_reduce_fusion.2
  74.7 7.2 fusion.21
  81.9 6.4 broadcast_in_dim.123.bias_ref
  88.4 49.9 %shard_map.162 = f32[8,2560]{1,0:T(8,128)} custom-call(s32[1]{0:T(128)} %bitcast.count_ref, s32[1,2560]{1,0:T(1,128)} %select_n.188.lab_ref, bf16[2560,768]{1,0:T(8,128)(2,1)} %get-tuple-element.30.tok_ref, bf16[12576,768]{1,0:T(8,128)(2,1)} %embed_ref.5, f32[12576,128]{1,0:T(8,128)} %broadcast_in_dim.123.bias_ref), custom_call_target="tpu_custom_call" | custom-call | flops 24999999488 | bytes 40000000 | tf_op jit(solution)/shard_map/pallas_call | solution.py:202
  138.2 0.9 slice.24
  139.2 24.6 %all-gather.1 = f32[16,4,2560]{2,1,0:T(4,128)S(1)} all-gather(f32[1,4,2560]{2,1,0:T(4,128)S(1)} %maximum_bitcast_fusion), channel_id=2, replica_groups=mesh['dp'=4,'tp'=4] {'dp','tp'}, dimensions={0}, use_global_device_ids=true | all-gather | bytes 696320 | tf_op jit(solution)/shard_map/all_gather | solution.py:263
  163.9 1.0 fusion.25
  168.5 127.8 %shard_map.163 = (f32[12576,768]{1,0:T(8,128)}, f32[12576,128]{1,0:T(8,128)}, f32[2560,768]{1,0:T(8,128)}) custom-call(s32[1]{0:T(128)} %bitcast.count_ref, s32[1,2560]{1,0:T(1,128)} %select_n.188.lab_ref, f32[4,2560]{1,0:T(4,128)} %get-tuple-element.42.meta_ref, bf16[2560,768]{1,0:T(8,128)(2,1)} %get-tuple-element.30.tok_ref, bf16[12576,768]{1,0:T(8,128)(2,1)} %embed_ref.5, ...), custom_call_target="tpu_custom_call" | custom-call | flops 74999996416 | bytes 40000000 | tf_op jit(solution)/shard_map/pallas_call | solution.py:202
  296.5 3.0 constant_dynamic-slice_fusion
  305.7 0.8 bitcast_dynamic-update-slice_fusion
  306.5 0.9 dynamic_update_slice.10
  307.4 0.7 dynamic_update_slice.11.meta_ref
  310.6 231.0 %all-reduce.4.cloned.1.call-done = f32[2560,768]{1,0:T(8,128)} async-done(((f32[2560,768]{1,0:T(8,128)}), f32[2560,768]{1,0:T(8,128)}) %all-reduce.4.cloned.1.call-update) | async-done | bytes 7864336 | tf_op jit(solution)/shard_map/psum | solution.py:289
  541.7 6.9 fusion.19
  548.7 0.8 copy-done.1
  549.4 6.6 multiply_reduce_fusion
  556.5 8.0 fusion.20
  564.5 1.9 copy-done.2
  566.4 6.7 fusion.9.rows_ref
  573.1 24.5 %shard_map.164 = bf16[32,512,768]{2,1,0:T(8,128)(2,1)} custom-call(s32[32]{0:T(128)} %get-tuple-element.36.base_ref, s32[32,1,128]{2,1,0:T(1,128)} %bitcast.82, f32[2560,768]{1,0:T(8,128)} %fusion.9.rows_ref), custom_call_target="tpu_custom_call" | custom-call | flops 8000000000 | bytes 40000000 | tf_op jit(solution)/shard_map/pallas_call | solution.py:202
  597.6 8.0 fusion.7
  605.6 17.4 %all-reduce = (f32[768]{0:T(1024)}, f32[768]{0:T(1024)}, f32[768]{0:T(1024)}) all-reduce(f32[768]{0:T(1024)S(1)} %get-tuple-element.27, f32[768]{0:T(1024)S(1)} %get-tuple-element.18, f32[768]{0:T(1024)S(1)} %get-tuple-element.20), channel_id=1, replica_groups=mesh['dp'=4,'tp'=4] {'dp'}, use_global_device_ids=true, to_apply=%region_17.18 | all-reduce | flops 2304 | bytes 18432 | tf_op jit(solution)/shard_map/psum | solution.py:323
  623.1 279.7 %shard_map.165 = (f32[12576,768]{1,0:T(8,128)}, f32[12576,128]{1,0:T(8,128)}) custom-call(s32[3]{0:T(128)} %pad_add_fusion.plan_ref, s32[30]{0:T(128)} %compare_select_fusion.6.src_ref, s32[30]{0:T(128)} %compare_select_fusion.5.dst_ref, s32[1,7936]{1,0:T(1,128)} %slice_convert_fusion.lab_ref, ...), custom_call_target="tpu_custom_call", output_to_operand_aliasing={{0}: (7, {})} | custom-call | flops 149999992832 | bytes 40000000 | tf_op jit(solution)/shard_map/pallas_call | solution.py:202
  902.8 6.6 add_reduce_fusion
  909.4 3.2 copy.65
  (101 shorter events, 10.9 us)
Async XLA Ops:
  8.0 533.7 %all-reduce.4.cloned.1.call-start = ((), (), s32[]{:S(2)}) async-start(), calls=%async_computation | async-start | bytes 15728640 | tf_op jit(solution)/shard_map/psum | solution.py:289
  17.6 27.9 %copy-start.24 = (f32[768]{0:T(1024)S(1)}, f32[768]{0:T(1024)}, u32[]{:S(2)}) copy-start(f32[768]{0:T(1024)} %param.15) | copy-start | bytes 9220
  69.1 3.1 copy-start
  69.1 5.6 copy-start.19
  69.1 5.6 copy-start.23
  69.1 12.8 %copy-start.4 = (f32[2560]{0:T(1024)}, f32[2560]{0:T(1024)S(1)}, u32[]{:S(2)}) copy-start(f32[2560]{0:T(1024)S(1)} %broadcast_multiply_fusion) | copy-start | bytes 30724
  74.7 7.2 copy-start.11
  74.7 7.2 copy-start.21
  165.7 2.8 copy-start.8
  166.7 1.7 copy-start.6
  167.1 0.7 copy-start.3
  296.3 3.3 copy-start.22
  296.3 7.9 copy-start.16
  296.3 8.0 copy-start.7
  296.3 8.0 copy-start.9
  296.3 8.0 copy-start.13
  296.4 10.1 %copy-start.15 = (f32[4,2560]{1,0:T(4,128)S(1)}, f32[4,2560]{1,0:T(4,128)}, u32[]{:S(2)}) copy-start(f32[4,2560]{1,0:T(4,128)} %get-tuple-element.41) | copy-start | bytes 122884
  296.4 11.0 %copy-start.14 = (f32[4,2560]{1,0:T(4,128)S(1)}, f32[4,2560]{1,0:T(4,128)}, u32[]{:S(2)}) copy-start(f32[4,2560]{1,0:T(4,128)} %get-tuple-element.40) | copy-start | bytes 122884
  296.4 245.3 %copy-start.5 = (f32[2560]{0:T(1024)S(1)}, f32[2560]{0:T(1024)}, u32[]{:S(2)}) copy-start(f32[2560]{0:T(1024)} %copy-done.4) | copy-start | bytes 30724
  296.4 245.3 %copy-start.20 = (f32[768]{0:T(1024)S(1)}, f32[768]{0:T(1024)}, u32[]{:S(2)}) copy-start(f32[768]{0:T(1024)} %param.16) | copy-start | bytes 9220
  296.4 326.6 %all-gather.4.cloned.1.call-start = ((), (), s32[]{:S(2)}) async-start(), calls=%async_computation.2 | async-start | bytes 33423360 | tf_op jit(solution)/shard_map/all_gather | solution.py:251
  299.5 609.8 %all-reduce.6.cloned.1.call-start = ((), (), s32[]{:S(2)}) async-start(), calls=%async_computation.1 | async-start | bytes 4718592 | tf_op jit(solution)/shard_map/psum | solution.py:323
  308.2 240.4 %copy-start.10 = (f32[4,7936]{1,0:T(4,128)}, f32[4,7936]{1,0:T(4,128)S(1)}, u32[]{:S(2)}) copy-start(f32[4,7936]{1,0:T(4,128)S(1)} %dynamic_update_slice.11.meta_ref) | copy-start | bytes 380932
  310.6 238.0 %copy-start.18 = (f32[2560]{0:T(1024)S(1)}, f32[2560]{0:T(1024)}, u32[]{:S(2)}) copy-start(f32[2560]{0:T(1024)} %copy-done.17) | copy-start | bytes 30724
  310.6 238.0 %copy-start.12 = (f32[2560]{0:T(1024)S(1)}, f32[2560]{0:T(1024)}, u32[]{:S(2)}) copy-start(f32[2560]{0:T(1024)} %copy-done.11) | copy-start | bytes 30724
  541.7 7.8 copy-start.1
  541.7 14.4 %slice-start = ((s8[7864320]{0:T(1024)(128)(4,1)}), s8[4194304]{0:T(1024)(128)(4,1)S(1)}, s32[]{:S(2)}) async-start(s8[7864320]{0:T(1024)(128)(4,1)} %bitcast.72), calls=%async_computation.3 | async-start | bytes 8388608
  541.7 14.4 %slice-start.2 = ((s8[7864320]{0:T(1024)(128)(4,1)}), s8[4194304]{0:T(1024)(128)(4,1)S(1)}, s32[]{:S(2)}) async-start(s8[7864320]{0:T(1024)(128)(4,1)} %bitcast.74), calls=%async_computation.5 | async-start | bytes 8388608
  549.4 6.6 slice-start.1
  549.4 7.0 slice-start.3
  549.4 7.0 copy-start.25
  564.5 1.9 copy-start.2
  (1 other events, 0.6 us)
Sparse Core Ops, SparseCore 0:
  296.5 245.0 all-reduce.3
  605.7 66.1 all-reduce.5
Sparse Core Ops, SparseCore 1:
  299.6 181.8 all-gather.3

commit v2 on v1

--- a/solution.py
+++ b/solution.py
@@ -6,6 +6,7 @@
 from jax.experimental import pallas as pl
 from jax.experimental.pallas import tpu as pltpu
 from jax.sharding import PartitionSpec as P
+
 
 LN_EPS = 1e-12
 LOSS_EPS = 1e-5
@@ -14,6 +15,8 @@
 CHUNK = 256
 STAGES = 4
 PICK = 96
+SEQS = 4
+SPLIT = 4
 OFF = 1e30
 VMEM_LIMIT = 67_000_000
 
@@ -44,48 +47,54 @@
 
 
 def pick_kernel(base_ref, idx_ref, hidden_ref, out_ref, acc):
-    seq = pl.program_id(0)
-
-    @pl.when(seq == 0)
+    step = pl.program_id(0)
+
+    @pl.when(step == 0)
     def _():
         acc[...] = jnp.zeros_like(acc)
 
-    rows = dot_tn(hot_rows(idx_ref[0], hidden_ref.shape[1]), hidden_ref[0])
-    base = pl.multiple_of(base_ref[seq], 8)
-    acc[pl.ds(base, 16), :] += rows[:16]
-    acc[pl.ds(base + 16, PICK - 16), :] = rows[16:]
-
-    @pl.when(seq == pl.num_programs(0) - 1)
+    picked = [dot_tn(hot_rows(idx_ref[k], hidden_ref.shape[1]), hidden_ref[k]) for k in range(SEQS)]
+    for k, rows in enumerate(picked):
+        base = pl.multiple_of(base_ref[step * SEQS + k], 8)
+        acc[pl.ds(base, 16), :] += rows[:16]
+        acc[pl.ds(base + 16, PICK - 16), :] = rows[16:]
+
+    @pl.when(step == pl.num_programs(0) - 1)
     def _():
         out_ref[...] = acc[...].astype(jnp.bfloat16)
 
 
 def place_kernel(base_ref, idx_ref, rows_ref, out_ref):
-    seq = pl.program_id(0)
-    base = pl.multiple_of(base_ref[seq], 8)
-    rows = rows_ref[pl.ds(base, PICK), :].astype(jnp.bfloat16)
-    out_ref[0] = dot_nn(hot_rows(idx_ref[0], out_ref.shape[1]), rows).astype(jnp.bfloat16)
+    step = pl.program_id(0)
+    for k in range(SEQS):
+        base = pl.multiple_of(base_ref[step * SEQS + k], 8)
+        rows = rows_ref[pl.ds(base, PICK), :].astype(jnp.bfloat16)
+        out_ref[k] = dot_nn(hot_rows(idx_ref[k], out_ref.shape[1]), rows).astype(jnp.bfloat16)
 
 
 def for_blocks(count, body):
     def pair(step, carry):
-        body(2 * step, 0)
-        body(2 * step + 1, 1)
+        body(pl.multiple_of(step * 2 * TOK, 2 * TOK), 2 * TOK)
         return carry
 
     lax.fori_loop(0, count // 2, pair, 0)
 
     @pl.when(count % 2 == 1)
     def _():
-        body(count - 1, 0)
-
-
-def tile_bias(bias_ref):
-    bias = bias_ref[...]
-    return jnp.concatenate([bias] * (TOK // bias.shape[1]), axis=1)
-
-
-def stats_kernel(count_ref, lab_ref, tok_ref, embed_ref, bias_ref, out_ref, z0, z1):
+        body(pl.multiple_of((count - 1) * TOK, TOK), TOK)
+
+
+def strips(height):
+    size = (height // 4 + 15) // 16 * 16
+    return [(at, min(size, height - at)) for at in range(0, height, size)]
+
+
+def tile_bias(bias_ref, at, size, width):
+    bias = bias_ref[at:at + size, :]
+    return jnp.concatenate([bias] * (width // bias.shape[1]), axis=1)
+
+
+def stats_kernel(count_ref, lab_ref, tok_ref, embed_ref, bias_ref, out_ref, z_ref):
     vblk = pl.program_id(0)
     height = embed_ref.shape[0]
 
@@ -94,40 +103,60 @@
         out_ref[...] = jnp.zeros_like(out_ref)
         out_ref[0:1, :] = jnp.full((1, out_ref.shape[1]), -jnp.inf, jnp.float32)
 
-    def body(block, slot):
-        z_ref = (z0, z1)[slot]
-        cols = pl.ds(pl.multiple_of(block * TOK, TOK), TOK)
-        z_ref[...] = dot_nt(embed_ref[...], tok_ref[cols, :]) + tile_bias(bias_ref)
+    def body(start, width):
+        cols = pl.ds(start, width)
+        tok = tok_ref[cols, :]
+        lab = lab_ref[0:1, cols] - vblk * height
+        parts = []
+        target = jnp.zeros((1, width), jnp.float32)
+        for at, size in strips(height):
+            z_ref[at:at + size, :width] = dot_nt(embed_ref[at:at + size, :], tok) + tile_bias(bias_ref, at, size, width)
+        for at, size in strips(height):
+            top = jnp.max(z_ref[at:at + size, :width], axis=0, keepdims=True)
+            total = jnp.sum(jnp.exp(z_ref[at:at + size, :width] - top), axis=0, keepdims=True)
+            hit = lax.broadcasted_iota(jnp.int32, (size, width), 0) == lab - at
+            target += jnp.sum(jnp.where(hit, z_ref[at:at + size, :width], 0.0), axis=0, keepdims=True)
+            parts.append((top, total))
         old_max = out_ref[0:1, cols]
-        new_max = jnp.maximum(old_max, jnp.max(z_ref[...], axis=0, keepdims=True))
-        part = jnp.sum(jnp.exp(z_ref[...] - new_max), axis=0, keepdims=True)
-        ids = lax.broadcasted_iota(jnp.int32, (height, TOK), 0)
-        hit = ids == lab_ref[0:1, cols] - vblk * height
-        target = jnp.sum(jnp.where(hit, z_ref[...], 0.0), axis=0, keepdims=True)
-        out_ref[1:2, cols] = out_ref[1:2, cols] * jnp.exp(old_max - new_max) + part
+        new_max = functools.reduce(jnp.maximum, [top for top, _ in parts], old_max)
+        total = out_ref[1:2, cols] * jnp.exp(old_max - new_max)
+        for top, part in parts:
+            total += part * jnp.exp(top - new_max)
         out_ref[0:1, cols] = new_max
+        out_ref[1:2, cols] = total
         out_ref[2:3, cols] += target
 
     for_blocks(count_ref[0], body)
 
 
-def logit_grad(vblk, block, tok, lab_ref, meta_ref, embed_ref, bias_ref, dbias_ref, z_ref, dz_ref):
-    cols = pl.ds(pl.multiple_of(block * TOK, TOK), TOK)
-    height = embed_ref.shape[0]
-    z_ref[...] = dot_nt(embed_ref[...], tok)
-    ids = lax.broadcasted_iota(jnp.int32, (height, TOK), 0)
-    hit = ids == lab_ref[0:1, cols] - vblk * height
-    probs = jnp.exp(z_ref[...] + tile_bias(bias_ref) - meta_ref[0:1, cols]) * meta_ref[1:2, cols]
-    dz = probs - jnp.where(hit, meta_ref[2:3, cols], 0.0)
-    lanes = dbias_ref.shape[1]
-    part = dz[:, :lanes]
-    for k in range(1, TOK // lanes):
-        part = part + dz[:, k * lanes:(k + 1) * lanes]
-    dbias_ref[...] += part
-    dz_ref[...] = dz.astype(jnp.bfloat16)
-
-
-def own_kernel(count_ref, lab_ref, meta_ref, tok_ref, embed_ref, bias_ref, dembed_ref, dbias_ref, dtok_ref, z0, z1, dz0, dz1):
+def logit_grad(vblk, start, width, tok_ref, lab_ref, meta_ref, embed_ref, bias_ref, dembed_ref, dbias_ref, z_ref, dz_ref):
+    cols = pl.ds(start, width)
+    height, lanes = embed_ref.shape[0], dbias_ref.shape[1]
+    tok = tok_ref[cols, :]
+    lab = lab_ref[0:1, cols] - vblk * height
+    top, scale, unit = meta_ref[0:1, cols], meta_ref[1:2, cols], meta_ref[2:3, cols]
+    todo = strips(height)
+
+    def logits(strip):
+        at, size = strip
+        z_ref[at:at + size, :width] = dot_nt(embed_ref[at:at + size, :], tok)
+
+    logits(todo[0])
+    for k, (at, size) in enumerate(todo):
+        if k + 1 < len(todo):
+            logits(todo[k + 1])
+        hit = lax.broadcasted_iota(jnp.int32, (size, width), 0) == lab - at
+        probs = jnp.exp(z_ref[at:at + size, :width] + tile_bias(bias_ref, at, size, width) - top) * scale
+        dz = probs - jnp.where(hit, unit, 0.0)
+        part = dz[:, :lanes]
+        for j in range(1, width // lanes):
+            part = part + dz[:, j * lanes:(j + 1) * lanes]
+        dbias_ref[at:at + size, :] += part
+        dz_ref[at:at + size, :width] = dz.astype(jnp.bfloat16)
+        dembed_ref[at:at + size, :] += dot_nn(dz_ref[at:at + size, :width], tok)
+
+
+def own_kernel(count_ref, lab_ref, meta_ref, tok_ref, embed_ref, bias_ref, dembed_ref, dbias_ref, dtok_ref, z_ref, dz_ref):
     vblk = pl.program_id(0)
 
     @pl.when(vblk == 0)
@@ -137,18 +166,14 @@
     dembed_ref[...] = jnp.zeros_like(dembed_ref)
     dbias_ref[...] = jnp.zeros_like(dbias_ref)
 
-    def body(block, slot):
-        z_ref, dz_ref = (z0, z1)[slot], (dz0, dz1)[slot]
-        rows = pl.ds(pl.multiple_of(block * TOK, TOK), TOK)
-        tok = tok_ref[rows, :]
-        logit_grad(vblk, block, tok, lab_ref, meta_ref, embed_ref, bias_ref, dbias_ref, z_ref, dz_ref)
-        dembed_ref[...] += dot_nn(dz_ref[...], tok)
-        dtok_ref[rows, :] += dot_tn(dz_ref[...], embed_ref[...])
+    def body(start, width):
+        logit_grad(vblk, start, width, tok_ref, lab_ref, meta_ref, embed_ref, bias_ref, dembed_ref, dbias_ref, z_ref, dz_ref)
+        dtok_ref[pl.ds(start, width), :] += dot_tn(dz_ref[:, :width], embed_ref[...])
 
     for_blocks(count_ref[0], body)
 
 
-def rest_kernel(plan_ref, src_ref, dst_ref, lab_ref, meta_ref, embed_ref, bias_ref, dembed_in_ref, tok_hbm, dembed_ref, dbias_ref, tok_ref, stage, sems, z0, z1, dz0, dz1):
+def rest_kernel(first, plan_ref, src_ref, dst_ref, lab_ref, meta_ref, embed_ref, bias_ref, dembed_in_ref, dbias_in_ref, tok_hbm, dembed_ref, dbias_ref, tok_ref, stage, sems, z_ref, dz_ref):
     vblk = pl.program_id(0)
     chunks = plan_ref[1]
 
@@ -161,10 +186,10 @@
     def _():
         end = pl.multiple_of(plan_ref[2], 16)
         tok_ref[pl.ds(end, TOK), :] = jnp.zeros((TOK, tok_ref.shape[1]), jnp.bfloat16)
-        for first in range(STAGES):
-            @pl.when(first < chunks)
+        for k in range(STAGES):
+            @pl.when(k < chunks)
             def _():
-                fetch(first).start()
+                fetch(k).start()
 
         def take(chunk, carry):
             fetch(chunk).wait()
@@ -174,18 +199,16 @@
             @pl.when(chunk + STAGES < chunks)
             def _():
                 fetch(chunk + STAGES).start()
+
             return carry
 
         lax.fori_loop(0, chunks, take, 0)
 
     dembed_ref[...] = dembed_in_ref[...]
-    dbias_ref[...] = jnp.zeros_like(dbias_ref)
-
-    def body(block, slot):
-        z_ref, dz_ref = (z0, z1)[slot], (dz0, dz1)[slot]
-        tok = tok_ref[pl.ds(pl.multiple_of(block * TOK, TOK), TOK), :]
-        logit_grad(vblk, block, tok, lab_ref, meta_ref, embed_ref, bias_ref, dbias_ref, z_ref, dz_ref)
-        dembed_ref[...] += dot_nn(dz_ref[...], tok)
+    dbias_ref[...] = dbias_in_ref[...]
+
+    def body(start, width):
+        logit_grad(vblk + first, start, width, tok_ref, lab_ref, meta_ref, embed_ref, bias_ref, dembed_ref, dbias_ref, z_ref, dz_ref)
 
     for_blocks(plan_ref[0], body)
 
@@ -194,8 +217,8 @@
     return pl.BlockSpec(shape, lambda *_: (0,) * len(shape))
 
 
-def by_rows(shape):
-    return pl.BlockSpec(shape, lambda step, *_: (step,) + (0,) * (len(shape) - 1))
+def by_rows(shape, first=0):
+    return pl.BlockSpec(shape, lambda step, *_: (step + first,) + (0,) * (len(shape) - 1))
 
 
 def run(kernel, scalars, grid, args, in_specs, out_specs, out_shape, scratch, flops, aliases=None):
@@ -239,8 +262,8 @@
         blocks = ((count + TOK - 1) // TOK).reshape(1)
 
         picked = run(
-            pick_kernel, (base,), batch, (idx_rows, hidden),
-            [by_rows((1, 1, 128)), by_rows((1, seq_len, width))], whole((rows, width)),
+            pick_kernel, (base,), batch // SEQS, (idx_rows, hidden),
+            [by_rows((SEQS, 1, 128)), by_rows((SEQS, seq_len, width))], whole((rows, width)),
             jax.ShapeDtypeStruct((rows, width), bf16), [pltpu.VMEM((rows, width), f32)], 8_000_000_000,
         )
         pre_act = jnp.dot(picked, w_t, preferred_element_type=f32) + b_t
@@ -252,8 +275,8 @@
 
         bias = jnp.broadcast_to(out_bias[:, None], (vocab, 128))
         local_lab = jnp.where(lab >= 0, lab - me_tp * vocab, -1)
-        z_scratch = [pltpu.VMEM((height, TOK), f32)] * 2
-        dz_scratch = [pltpu.VMEM((height, TOK), bf16)] * 2
+        z_scratch = [pltpu.VMEM((height, 2 * TOK), f32)]
+        dz_scratch = [pltpu.VMEM((height, 2 * TOK), bf16)]
         stats = run(
             stats_kernel, (blocks,), VOCAB_BLOCKS, (local_lab[None, :], tok, embed, bias),
             [whole((1, rows)), whole((rows, width)), by_rows((height, width)), by_rows((height, 128))], whole((8, rows)),
@@ -306,25 +329,29 @@
             pos = pos + (size + 15) // 16 * 16
         plan = jnp.stack([(pos + TOK - 1) // TOK, chunks, last])
         meta_lab = meta[3:4].astype(i32)
-        d_embed, d_bias_rest = run(
-            rest_kernel, (plan, src, dst), VOCAB_BLOCKS, (meta_lab, meta, embed, bias, d_embed, tok_all),
-            [whole((1, cap + TOK)), whole((4, cap + TOK)), by_rows((height, width)), by_rows((height, 128)), by_rows((height, width)), pl.BlockSpec(memory_space=pl.ANY)],
-            [by_rows((height, width)), by_rows((height, 128))],
-            [jax.ShapeDtypeStruct((vocab, width), f32), jax.ShapeDtypeStruct((vocab, 128), f32)],
-            [pltpu.VMEM((cap + TOK, width), bf16), pltpu.VMEM((STAGES, CHUNK, width), f32), pltpu.SemaphoreType.DMA((STAGES,))] + z_scratch + dz_scratch,
-            150_000_000_000, {7: 0},
-        )
-        d_out_bias = jnp.sum(d_bias_own + d_bias_rest, axis=1)
+        d_bias = d_bias_own
+        for first, last_blk in ((0, SPLIT), (SPLIT, VOCAB_BLOCKS)):
+            blk = functools.partial(by_rows, first=first)
+            d_embed, d_bias = run(
+                functools.partial(rest_kernel, first), (plan, src, dst), last_blk - first, (meta_lab, meta, embed, bias, d_embed, d_bias, tok_all),
+                [whole((1, cap + TOK)), whole((4, cap + TOK)), blk((height, width)), blk((height, 128)), blk((height, width)), blk((height, 128)), pl.BlockSpec(memory_space=pl.ANY)],
+                [blk((height, width)), blk((height, 128))],
+                [jax.ShapeDtypeStruct((vocab, width), f32), jax.ShapeDtypeStruct((vocab, 128), f32)],
+                [pltpu.VMEM((cap + TOK, width), bf16), pltpu.VMEM((STAGES, CHUNK, width), f32), pltpu.SemaphoreType.DMA((STAGES,))] + z_scratch + dz_scratch,
+                25_000_000_000 * (last_blk - first), {7: 0, 8: 1},
+            )
+        d_out_bias = jnp.sum(d_bias, axis=1)
 
         d_pre, d_gamma, d_beta = norm_vjp(d_normed)
         d_pre_bf = d_pre.astype(bf16)
         d_w_t = jnp.einsum("nd,ne->de", picked, d_pre_bf, preferred_element_type=f32)
         d_b_t = jnp.sum(d_pre, axis=0)
-        d_w_t, d_b_t, d_gamma, d_beta = lax.psum((d_w_t, d_b_t, d_gamma, d_beta), "dp")
+        d_w_t = lax.psum(d_w_t, "dp")
+        d_b_t, d_gamma, d_beta = lax.psum((d_b_t, d_gamma, d_beta), "dp")
         d_rows = jnp.einsum("ne,de->nd", d_pre_bf, w_t, preferred_element_type=f32)
         d_hidden = run(
-            place_kernel, (base,), batch, (idx_rows, d_rows),
-            [by_rows((1, 1, 128)), whole((rows, width))], by_rows((1, seq_len, width)),
+            place_kernel, (base,), batch // SEQS, (idx_rows, d_rows),
+            [by_rows((SEQS, 1, 128)), whole((rows, width))], by_rows((SEQS, seq_len, width)),
             jax.ShapeDtypeStruct((batch, seq_len, width), bf16), [], 8_000_000_000,
         )
         return loss, d_hidden, d_w_t, d_b_t, d_gamma, d_beta, d_embed, d_out_bias

time: 932 us -> 821 us (0.88)
  the two profiles are of different devices: /device:TPU:0 before, /device:TPU:4 now
where the time goes in v2:
time: 821 us; the launch traced here: 811 us
  Pallas kernels  402 us (49%)
  waiting for transfers between devices  237 us (29%)
  other arithmetic  49.4 us (6%)
  matrix products  38.2 us (5%)
  blocking collectives  35.2 us (4%)
  local copies, waits for them, and re-layouts  25.9 us (3%)
  between operations  23.5 us (3%)
    pallas_call x6, Pallas kernels, run(): pl.pallas_call(kernel, grid_spec=pltpu.PrefetchScalarGridSpec(num_scalar_...  402 us
    psum x1, waiting for transfers between devices, local_step(): d_normed = lax.psum(d_tok, 'tp')  237 us
    dot_general x1, matrix products, local_step(): pre_act = jnp.dot(picked, w_t, preferred_element_type=f32) + b_t  23.5 us
    all_gather x1, blocking collectives, local_step(): lax.all_gather(packet, ('dp', 'tp')).reshape(groups, shards, 4, rows)  19.5 us
  transfers between devices with their start and end apart: 3, of which 1 were waited for; matrix products, arithmetic and copies ran while one was open for 6% of the time, Pallas kernels for 28%

profile of v2, /device:TPU:4, one launch (start us, length us, event | category | flops | bytes accessed | tf_op | source)
XLA Modules:
  0.0 811.1 jit_solution(13736928764459069970)
XLA Ops:
  8.1 0.8 reduce_sum.180
  9.0 1.2 fusion.24
  12.4 1.0 select_reduce_fusion.1
  14.1 2.9 select_reduce_fusion
  17.6 15.4 %shard_map.161 = bf16[2560,768]{1,0:T(8,128)(2,1)} custom-call(s32[32]{0:T(128)} %get-tuple-element.40.base_ref, s32[32,1,128]{2,1,0:T(1,128)} %bitcast.81, bf16[32,512,768]{2,1,0:T(8,128)(2,1)} %hidden_ref.1), custom_call_target="tpu_custom_call" | custom-call | flops 8000000000 | bytes 40000000 | tf_op jit(solution)/shard_map/pallas_call | solution.py:225
  33.0 23.5 %fusion.22 = (f32[2560]{0:T(1024)S(1)}, f32[2560,768]{1,0:T(8,128)S(1)}, f32[2560,768]{1,0:T(8,128)}, f32[2560,768]{1,0:T(8,128)}) fusion(f32[768]{0:T(1024)S(1)} %copy-done.24, bf16[2560,768]{1,0:T(8,128)(2,1)} %shard_map.161, bf16[768,768]{1,0:T(8,128)(2,1)} %param.14), kind=kOutput, calls=%fused_computation.90 | convolution fusion | flops 3149657600 | bytes 28718080 | tf_op jit(solution)/shard_map/dot_general | solution.py:269
  56.6 3.1 copy-done
  59.7 1.8 multiply_reduce_fusion.2
  62.2 7.2 fusion.21
  69.4 6.4 broadcast_in_dim.123.bias_ref
  75.8 44.0 %shard_map.162 = f32[8,2560]{1,0:T(8,128)} custom-call(s32[1]{0:T(128)} %bitcast.count_ref, s32[1,2560]{1,0:T(1,128)} %select_n.188.lab_ref, bf16[2560,768]{1,0:T(8,128)(2,1)} %get-tuple-element.34.tok_ref, bf16[12576,768]{1,0:T(8,128)(2,1)} %embed_ref.7, f32[12576,128]{1,0:T(8,128)} %broadcast_in_dim.123.bias_ref), custom_call_target="tpu_custom_call" | custom-call | flops 24999999488 | bytes 40000000 | tf_op jit(solution)/shard_map/pallas_call | solution.py:225
  119.8 0.9 slice.24
  120.7 19.5 %all-gather.1 = f32[16,4,2560]{2,1,0:T(4,128)S(1)} all-gather(f32[1,4,2560]{2,1,0:T(4,128)S(1)} %maximum_bitcast_fusion), channel_id=2, replica_groups=mesh['dp'=4,'tp'=4] {'dp','tp'}, dimensions={0}, use_global_device_ids=true | all-gather | bytes 696320 | tf_op jit(solution)/shard_map/all_gather | solution.py:286
  140.4 1.0 fusion.25
  144.9 112.0 %shard_map.163 = (f32[12576,768]{1,0:T(8,128)}, f32[12576,128]{1,0:T(8,128)}, f32[2560,768]{1,0:T(8,128)}) custom-call(s32[1]{0:T(128)} %bitcast.count_ref, s32[1,2560]{1,0:T(1,128)} %select_n.188.lab_ref, f32[4,2560]{1,0:T(4,128)} %get-tuple-element.46.meta_ref, bf16[2560,768]{1,0:T(8,128)(2,1)} %get-tuple-element.34.tok_ref, bf16[12576,768]{1,0:T(8,128)(2,1)} %embed_ref.7, ...), custom_call_target="tpu_custom_call" | custom-call | flops 74999996416 | bytes 40000000 | tf_op jit(solution)/shard_map/pallas_call | solution.py:225
  257.1 3.0 constant_dynamic-slice_fusion
  266.3 0.8 bitcast_dynamic-update-slice_fusion
  267.1 1.1 dynamic_update_slice.10
  271.5 236.7 %all-reduce.4.cloned.1.call-done = f32[2560,768]{1,0:T(8,128)} async-done(((f32[2560,768]{1,0:T(8,128)}), f32[2560,768]{1,0:T(8,128)}) %all-reduce.4.cloned.1.call-update) | async-done | bytes 7864336 | tf_op jit(solution)/shard_map/psum | solution.py:312
  508.2 6.9 fusion.19
  515.2 0.8 copy-done.1
  516.0 6.6 multiply_reduce_fusion
  523.0 8.0 fusion.20
  531.0 1.9 copy-done.2
  532.9 6.7 fusion.9.rows_ref
  539.6 15.5 %shard_map.164 = bf16[32,512,768]{2,1,0:T(8,128)(2,1)} custom-call(s32[32]{0:T(128)} %get-tuple-element.40.base_ref, s32[32,1,128]{2,1,0:T(1,128)} %bitcast.82, f32[2560,768]{1,0:T(8,128)} %fusion.9.rows_ref), custom_call_target="tpu_custom_call" | custom-call | flops 8000000000 | bytes 40000000 | tf_op jit(solution)/shard_map/pallas_call | solution.py:225
  555.1 8.0 fusion.7
  563.1 15.7 %all-reduce = (f32[768]{0:T(1024)}, f32[768]{0:T(1024)}, f32[768]{0:T(1024)}) all-reduce(f32[768]{0:T(1024)S(1)} %get-tuple-element.31, f32[768]{0:T(1024)S(1)} %get-tuple-element.22, f32[768]{0:T(1024)S(1)} %get-tuple-element.24), channel_id=1, replica_groups=mesh['dp'=4,'tp'=4] {'dp'}, use_global_device_ids=true, to_apply=%region_17.18 | all-reduce | flops 2304 | bytes 18432 | tf_op jit(solution)/shard_map/psum | solution.py:350
  578.8 137.8 %shard_map.165 = (f32[12576,768]{1,0:T(8,128)}, f32[12576,128]{1,0:T(8,128)}) custom-call(s32[3]{0:T(128)} %pad_add_fusion.plan_ref, s32[30]{0:T(128)} %compare_select_fusion.6.src_ref, s32[30]{0:T(128)} %compare_select_fusion.5.dst_ref, s32[1,7936]{1,0:T(1,128)} %slice_convert_fusion.lab_ref, ...), custom_call_target="tpu_custom_call", output_to_operand_aliasing={{0}: (7, {}), {1}: (8, {})} | custom-call | flops 99999997952 | bytes 40000000 | tf_op jit(solution)/shard_map/pallas_call | solution.py:225
  716.6 77.3 %shard_map.166 = (f32[12576,768]{1,0:T(8,128)}, f32[12576,128]{1,0:T(8,128)}) custom-call(s32[3]{0:T(128)} %pad_add_fusion.plan_ref, s32[30]{0:T(128)} %compare_select_fusion.6.src_ref, s32[30]{0:T(128)} %compare_select_fusion.5.dst_ref, s32[1,7936]{1,0:T(1,128)} %slice_convert_fusion.lab_ref, ...), custom_call_target="tpu_custom_call", output_to_operand_aliasing={{0}: (7, {}), {1}: (8, {})} | custom-call | flops 49999998976 | bytes 40000000 | tf_op jit(solution)/shard_map/pallas_call | solution.py:225
  794.0 5.1 reduce_sum.198
  799.1 3.2 copy.71
  (102 shorter events, 11.6 us)
Async XLA Ops:
  8.0 500.2 %all-reduce.4.cloned.1.call-start = ((), (), s32[]{:S(2)}) async-start(), calls=%async_computation | async-start | bytes 15728640 | tf_op jit(solution)/shard_map/psum | solution.py:312
  17.6 15.4 %copy-start.24 = (f32[768]{0:T(1024)S(1)}, f32[768]{0:T(1024)}, u32[]{:S(2)}) copy-start(f32[768]{0:T(1024)} %param.15) | copy-start | bytes 9220
  56.6 3.1 copy-start
  56.6 5.6 copy-start.19
  56.6 5.6 copy-start.23
  56.6 12.8 %copy-start.4 = (f32[2560]{0:T(1024)}, f32[2560]{0:T(1024)S(1)}, u32[]{:S(2)}) copy-start(f32[2560]{0:T(1024)S(1)} %broadcast_multiply_fusion) | copy-start | bytes 30724
  62.1 7.2 copy-start.11
  62.2 7.2 copy-start.21
  142.1 2.8 copy-start.8
  143.2 1.7 copy-start.6
  143.6 0.7 copy-start.3
  257.0 3.3 copy-start.22
  257.0 7.9 copy-start.16
  257.0 8.0 copy-start.7
  257.0 8.0 copy-start.9
  257.0 8.0 copy-start.13
  257.0 10.1 %copy-start.15 = (f32[4,2560]{1,0:T(4,128)S(1)}, f32[4,2560]{1,0:T(4,128)}, u32[]{:S(2)}) copy-start(f32[4,2560]{1,0:T(4,128)} %get-tuple-element.45) | copy-start | bytes 122884
  257.0 11.2 %copy-start.14 = (f32[4,2560]{1,0:T(4,128)S(1)}, f32[4,2560]{1,0:T(4,128)}, u32[]{:S(2)}) copy-start(f32[4,2560]{1,0:T(4,128)} %get-tuple-element.44) | copy-start | bytes 122884
  257.0 251.1 %copy-start.5 = (f32[2560]{0:T(1024)S(1)}, f32[2560]{0:T(1024)}, u32[]{:S(2)}) copy-start(f32[2560]{0:T(1024)} %copy-done.4) | copy-start | bytes 30724
  257.0 251.1 %copy-start.20 = (f32[768]{0:T(1024)S(1)}, f32[768]{0:T(1024)}, u32[]{:S(2)}) copy-start(f32[768]{0:T(1024)} %param.16) | copy-start | bytes 9220
  257.1 321.7 %all-gather.4.cloned.1.call-start = ((), (), s32[]{:S(2)}) async-start(), calls=%async_computation.2 | async-start | bytes 33423360 | tf_op jit(solution)/shard_map/all_gather | solution.py:274
  260.2 538.9 %all-reduce.6.cloned.1.call-start = ((), (), s32[]{:S(2)}) async-start(), calls=%async_computation.1 | async-start | bytes 4718592 | tf_op jit(solution)/shard_map/psum | solution.py:349
  269.0 246.1 %copy-start.10 = (f32[4,7936]{1,0:T(4,128)}, f32[4,7936]{1,0:T(4,128)S(1)}, u32[]{:S(2)}) copy-start(f32[4,7936]{1,0:T(4,128)S(1)} %dynamic_update_slice.11.meta_ref) | copy-start | bytes 380932
  271.5 243.7 %copy-start.18 = (f32[2560]{0:T(1024)S(1)}, f32[2560]{0:T(1024)}, u32[]{:S(2)}) copy-start(f32[2560]{0:T(1024)} %copy-done.17) | copy-start | bytes 30724
  271.5 243.7 %copy-start.12 = (f32[2560]{0:T(1024)S(1)}, f32[2560]{0:T(1024)}, u32[]{:S(2)}) copy-start(f32[2560]{0:T(1024)} %copy-done.11) | copy-start | bytes 30724
  508.2 7.8 copy-start.1
  508.2 14.4 %slice-start = ((s8[7864320]{0:T(1024)(128)(4,1)}), s8[4194304]{0:T(1024)(128)(4,1)S(1)}, s32[]{:S(2)}) async-start(s8[7864320]{0:T(1024)(128)(4,1)} %bitcast.72), calls=%async_computation.3 | async-start | bytes 8388608
  508.2 14.4 %slice-start.2 = ((s8[7864320]{0:T(1024)(128)(4,1)}), s8[4194304]{0:T(1024)(128)(4,1)S(1)}, s32[]{:S(2)}) async-start(s8[7864320]{0:T(1024)(128)(4,1)} %bitcast.74), calls=%async_computation.5 | async-start | bytes 8388608
  516.0 6.6 slice-start.1
  516.0 7.0 slice-start.3
  516.0 7.0 copy-start.25
  531.0 1.9 copy-start.2
  (1 other events, 0.6 us)
Sparse Core Ops, SparseCore 0:
  257.2 250.9 all-reduce.3
  563.2 66.7 all-reduce.5
Sparse Core Ops, SparseCore 1:
  260.3 187.4 all-gather.3

commit v3 on v2

--- a/solution.py
+++ b/solution.py
@@ -74,14 +74,14 @@
 
 def for_blocks(count, body):
     def pair(step, carry):
-        body(pl.multiple_of(step * 2 * TOK, 2 * TOK), 2 * TOK)
+        body(step, 2 * TOK)
         return carry
 
     lax.fori_loop(0, count // 2, pair, 0)
 
     @pl.when(count % 2 == 1)
     def _():
-        body(pl.multiple_of((count - 1) * TOK, TOK), TOK)
+        body(count // 2, TOK)
 
 
 def strips(height):
@@ -94,28 +94,40 @@
     return jnp.concatenate([bias] * (width // bias.shape[1]), axis=1)
 
 
-def stats_kernel(count_ref, lab_ref, tok_ref, embed_ref, bias_ref, out_ref, z_ref):
+def stats_kernel(count_ref, lab_ref, tok_ref, embed_ref, bias_ref, out_ref, logits_hbm, z_ref, sems):
     vblk = pl.program_id(0)
     height = embed_ref.shape[0]
+    steps = (count_ref[0] + 1) // 2
+
+    def save(vocab_blk, step, slot):
+        return pltpu.make_async_copy(z_ref.at[slot], logits_hbm.at[vocab_blk, step], sems.at[slot])
 
     @pl.when(vblk == 0)
     def _():
         out_ref[...] = jnp.zeros_like(out_ref)
         out_ref[0:1, :] = jnp.full((1, out_ref.shape[1]), -jnp.inf, jnp.float32)
 
-    def body(start, width):
-        cols = pl.ds(start, width)
+    def body(step, width):
+        cols = pl.ds(pl.multiple_of(step * 2 * TOK, 2 * TOK), width)
+        turn = vblk * steps + step
+        slot = lax.rem(turn, 2)
+
+        @pl.when(turn >= 2)
+        def _():
+            save(vblk, step, slot).wait()
+
         tok = tok_ref[cols, :]
         lab = lab_ref[0:1, cols] - vblk * height
         parts = []
         target = jnp.zeros((1, width), jnp.float32)
         for at, size in strips(height):
-            z_ref[at:at + size, :width] = dot_nt(embed_ref[at:at + size, :], tok) + tile_bias(bias_ref, at, size, width)
+            z_ref[slot, at:at + size, :width] = dot_nt(embed_ref[at:at + size, :], tok) + tile_bias(bias_ref, at, size, width)
         for at, size in strips(height):
-            top = jnp.max(z_ref[at:at + size, :width], axis=0, keepdims=True)
-            total = jnp.sum(jnp.exp(z_ref[at:at + size, :width] - top), axis=0, keepdims=True)
+            z = z_ref[slot, at:at + size, :width]
+            top = jnp.max(z, axis=0, keepdims=True)
+            total = jnp.sum(jnp.exp(z - top), axis=0, keepdims=True)
             hit = lax.broadcasted_iota(jnp.int32, (size, width), 0) == lab - at
-            target += jnp.sum(jnp.where(hit, z_ref[at:at + size, :width], 0.0), axis=0, keepdims=True)
+            target += jnp.sum(jnp.where(hit, z, 0.0), axis=0, keepdims=True)
             parts.append((top, total))
         old_max = out_ref[0:1, cols]
         new_max = functools.reduce(jnp.maximum, [top for top, _ in parts], old_max)
@@ -125,50 +137,73 @@
         out_ref[0:1, cols] = new_max
         out_ref[1:2, cols] = total
         out_ref[2:3, cols] += target
+        save(vblk, step, slot).start()
 
     for_blocks(count_ref[0], body)
 
-
-def logit_grad(vblk, start, width, tok_ref, lab_ref, meta_ref, embed_ref, bias_ref, dembed_ref, dbias_ref, z_ref, dz_ref):
-    cols = pl.ds(start, width)
-    height, lanes = embed_ref.shape[0], dbias_ref.shape[1]
-    tok = tok_ref[cols, :]
-    lab = lab_ref[0:1, cols] - vblk * height
-    top, scale, unit = meta_ref[0:1, cols], meta_ref[1:2, cols], meta_ref[2:3, cols]
-    todo = strips(height)
-
-    def logits(strip):
-        at, size = strip
-        z_ref[at:at + size, :width] = dot_nt(embed_ref[at:at + size, :], tok)
-
-    logits(todo[0])
-    for k, (at, size) in enumerate(todo):
-        if k + 1 < len(todo):
-            logits(todo[k + 1])
-        hit = lax.broadcasted_iota(jnp.int32, (size, width), 0) == lab - at
-        probs = jnp.exp(z_ref[at:at + size, :width] + tile_bias(bias_ref, at, size, width) - top) * scale
-        dz = probs - jnp.where(hit, unit, 0.0)
-        part = dz[:, :lanes]
-        for j in range(1, width // lanes):
-            part = part + dz[:, j * lanes:(j + 1) * lanes]
-        dbias_ref[at:at + size, :] += part
-        dz_ref[at:at + size, :width] = dz.astype(jnp.bfloat16)
-        dembed_ref[at:at + size, :] += dot_nn(dz_ref[at:at + size, :width], tok)
-
-
-def own_kernel(count_ref, lab_ref, meta_ref, tok_ref, embed_ref, bias_ref, dembed_ref, dbias_ref, dtok_ref, z_ref, dz_ref):
+    @pl.when(vblk == pl.num_programs(0) - 1)
+    def _():
+        turns = pl.num_programs(0) * steps
+        save(0, 0, lax.rem(turns, 2)).wait()
+        save(0, 0, lax.rem(turns + 1, 2)).wait()
+
+
+def grad_strip(at, size, width, z, lab, top, scale, unit, dbias_ref, dz_ref, fresh=None):
+    lanes = dbias_ref.shape[1]
+    hit = lax.broadcasted_iota(jnp.int32, (size, width), 0) == lab - at
+    dz = jnp.exp(z - top) * scale - jnp.where(hit, unit, 0.0)
+    part = dz[:, :lanes]
+    for j in range(1, width // lanes):
+        part = part + dz[:, j * lanes:(j + 1) * lanes]
+    old = dbias_ref[at:at + size, :]
+    dbias_ref[at:at + size, :] = part + (old if fresh is None else jnp.where(fresh, 0.0, old))
+    dz_ref[at:at + size, :width] = dz.astype(jnp.bfloat16)
+
+
+def token_row(cols, vblk, height, lab_ref, meta_ref):
+    return lab_ref[0:1, cols] - vblk * height, meta_ref[0:1, cols], meta_ref[1:2, cols], meta_ref[2:3, cols]
+
+
+def own_kernel(count_ref, lab_ref, meta_ref, tok_ref, embed_ref, logits_hbm, dembed_ref, dbias_ref, dtok_ref, z_ref, sems, dz_ref):
     vblk = pl.program_id(0)
+    height = embed_ref.shape[0]
+    steps = (count_ref[0] + 1) // 2
+
+    def load(vocab_blk, step, slot):
+        return pltpu.make_async_copy(logits_hbm.at[vocab_blk, step], z_ref.at[slot], sems.at[slot])
 
     @pl.when(vblk == 0)
     def _():
         dtok_ref[...] = jnp.zeros_like(dtok_ref)
-
-    dembed_ref[...] = jnp.zeros_like(dembed_ref)
-    dbias_ref[...] = jnp.zeros_like(dbias_ref)
-
-    def body(start, width):
-        logit_grad(vblk, start, width, tok_ref, lab_ref, meta_ref, embed_ref, bias_ref, dembed_ref, dbias_ref, z_ref, dz_ref)
-        dtok_ref[pl.ds(start, width), :] += dot_tn(dz_ref[:, :width], embed_ref[...])
+        load(0, 0, 0).start()
+
+    def body(step, width):
+        turn = vblk * steps + step
+        slot = lax.rem(turn, 2)
+        wrap = step + 1 == steps
+        next_blk, next_step = jnp.where(wrap, vblk + 1, vblk), jnp.where(wrap, 0, step + 1)
+
+        @pl.when(next_blk < pl.num_programs(0))
+        def _():
+            load(next_blk, next_step, 1 - slot).start()
+
+        load(vblk, step, slot).wait()
+        cols = pl.ds(pl.multiple_of(step * 2 * TOK, 2 * TOK), width)
+        tok = tok_ref[cols, :]
+        row = token_row(cols, vblk, height, lab_ref, meta_ref)
+        fresh = step == 0
+        todo = strips(height)
+
+        def grad(at, size):
+            grad_strip(at, size, width, z_ref[slot, at:at + size, :width], *row, dbias_ref, dz_ref, fresh)
+
+        grad(*todo[0])
+        for k, (at, size) in enumerate(todo):
+            if k + 1 < len(todo):
+                grad(*todo[k + 1])
+            dz = dz_ref[at:at + size, :width]
+            dembed_ref[at:at + size, :] = dot_nn(dz, tok) + jnp.where(fresh, 0.0, dembed_ref[at:at + size, :])
+        dtok_ref[cols, :] += dot_tn(dz_ref[:, :width], embed_ref[...])
 
     for_blocks(count_ref[0], body)
 
@@ -207,8 +242,23 @@
     dembed_ref[...] = dembed_in_ref[...]
     dbias_ref[...] = dbias_in_ref[...]
 
-    def body(start, width):
-        logit_grad(vblk + first, start, width, tok_ref, lab_ref, meta_ref, embed_ref, bias_ref, dembed_ref, dbias_ref, z_ref, dz_ref)
+    height = embed_ref.shape[0]
+
+    def body(step, width):
+        cols = pl.ds(pl.multiple_of(step * 2 * TOK, 2 * TOK), width)
+        tok = tok_ref[cols, :]
+        row = token_row(cols, vblk + first, height, lab_ref, meta_ref)
+        todo = strips(height)
+
+        def logits(at, size):
+            z_ref[at:at + size, :width] = dot_nt(embed_ref[at:at + size, :], tok)
+
+        logits(*todo[0])
+        for k, (at, size) in enumerate(todo):
+            if k + 1 < len(todo):
+                logits(*todo[k + 1])
+            grad_strip(at, size, width, z_ref[at:at + size, :width] + tile_bias(bias_ref, at, size, width), *row, dbias_ref, dz_ref)
+            dembed_ref[at:at + size, :] += dot_nn(dz_ref[at:at + size, :width], tok)
 
     for_blocks(plan_ref[0], body)
 
@@ -277,10 +327,13 @@
         local_lab = jnp.where(lab >= 0, lab - me_tp * vocab, -1)
         z_scratch = [pltpu.VMEM((height, 2 * TOK), f32)]
         dz_scratch = [pltpu.VMEM((height, 2 * TOK), bf16)]
-        stats = run(
+        logit_shape = (VOCAB_BLOCKS, -(-rows // (2 * TOK)), height, 2 * TOK)
+        slots_scratch = [pltpu.VMEM((2, height, 2 * TOK), f32), pltpu.SemaphoreType.DMA((2,))]
+        anywhere = pl.BlockSpec(memory_space=pl.ANY)
+        stats, logits = run(
             stats_kernel, (blocks,), VOCAB_BLOCKS, (local_lab[None, :], tok, embed, bias),
-            [whole((1, rows)), whole((rows, width)), by_rows((height, width)), by_rows((height, 128))], whole((8, rows)),
-            jax.ShapeDtypeStruct((8, rows), f32), z_scratch, 25_000_000_000,
+            [whole((1, rows)), whole((rows, width)), by_rows((height, width)), by_rows((height, 128))], [whole((8, rows)), anywhere],
+            [jax.ShapeDtypeStruct((8, rows), f32), jax.ShapeDtypeStruct(logit_shape, f32)], slots_scratch, 25_000_000_000,
         )
         packet = jnp.concatenate([stats[:3], lab.astype(f32)[None, :]], axis=0)
         packets = lax.all_gather(packet, ("dp", "tp")).reshape(groups, shards, 4, rows)
@@ -303,11 +356,11 @@
 
         own_meta = lax.dynamic_index_in_dim(metas, me_dp, 0, keepdims=False)
         d_embed, d_bias_own, d_tok = run(
-            own_kernel, (blocks,), VOCAB_BLOCKS, (local_lab[None, :], own_meta, tok, embed, bias),
-            [whole((1, rows)), whole((4, rows)), whole((rows, width)), by_rows((height, width)), by_rows((height, 128))],
+            own_kernel, (blocks,), VOCAB_BLOCKS, (local_lab[None, :], own_meta, tok, embed, logits),
+            [whole((1, rows)), whole((4, rows)), whole((rows, width)), by_rows((height, width)), anywhere],
             [by_rows((height, width)), by_rows((height, 128)), whole((rows, width))],
             [jax.ShapeDtypeStruct((vocab, width), f32), jax.ShapeDtypeStruct((vocab, 128), f32), jax.ShapeDtypeStruct((rows, width), f32)],
-            z_scratch + dz_scratch, 75_000_000_000,
+            slots_scratch + dz_scratch, 50_000_000_000,
         )
         d_normed = lax.psum(d_tok, "tp")
 
@@ -346,8 +399,9 @@
         d_pre_bf = d_pre.astype(bf16)
         d_w_t = jnp.einsum("nd,ne->de", picked, d_pre_bf, preferred_element_type=f32)
         d_b_t = jnp.sum(d_pre, axis=0)
-        d_w_t = lax.psum(d_w_t, "dp")
-        d_b_t, d_gamma, d_beta = lax.psum((d_b_t, d_gamma, d_beta), "dp")
+        small = jnp.stack([d_b_t, d_gamma, d_beta] + [jnp.zeros_like(d_b_t)] * 5)
+        sums = lax.psum(jnp.concatenate([d_w_t, small], axis=0), "dp")
+        d_w_t, d_b_t, d_gamma, d_beta = sums[:width], sums[width], sums[width + 1], sums[width + 2]
         d_rows = jnp.einsum("ne,de->nd", d_pre_bf, w_t, preferred_element_type=f32)
         d_hidden = run(
             place_kernel, (base,), batch // SEQS, (idx_rows, d_rows),

time: 821 us -> 806 us (0.982)
  the two profiles are of different devices: /device:TPU:4 before, /device:TPU:0 now
where the time goes in v3:
time: 806 us; the launch traced here: 793 us
  Pallas kernels  386 us (48%)
  waiting for transfers between devices  244 us (30%)
  other arithmetic  50.3 us (6%)
  matrix products  40.4 us (5%)
  local copies, waits for them, and re-layouts  32.4 us (4%)
  between operations  23.6 us (3%)
  blocking collectives  15.8 us (2%)
    pallas_call x6, Pallas kernels, run(): pl.pallas_call(kernel, grid_spec=pltpu.PrefetchScalarGridSpec(num_scalar_...  386 us
    psum x1, waiting for transfers between devices, local_step(): d_normed = lax.psum(d_tok, 'tp')  141 us
    psum x1, waiting for transfers between devices, local_step(): sums = lax.psum(jnp.concatenate([d_w_t, small], axis=0), 'dp')  104 us
    dot_general x1, matrix products, local_step(): pre_act = jnp.dot(picked, w_t, preferred_element_type=f32) + b_t  23.5 us
  transfers between devices with their start and end apart: 3, of which 2 were waited for; matrix products, arithmetic and copies ran while one was open for 3% of the time, Pallas kernels for 2%

profile of v3, /device:TPU:0, one launch (start us, length us, event | category | flops | bytes accessed | tf_op | source)
XLA Modules:
  0.0 792.9 jit_solution(3715061873849032695)
XLA Ops:
  8.0 0.8 reduce_sum.180
  9.0 1.2 fusion.24
  11.8 2.9 select_reduce_fusion
  16.0 1.5 select_reduce_fusion.1
  18.1 15.4 %shard_map.161 = bf16[2560,768]{1,0:T(8,128)(2,1)} custom-call(s32[32]{0:T(128)} %get-tuple-element.44.base_ref, s32[32,1,128]{2,1,0:T(1,128)} %bitcast.81, bf16[32,512,768]{2,1,0:T(8,128)(2,1)} %hidden_ref.1), custom_call_target="tpu_custom_call" | custom-call | flops 8000000000 | bytes 40000000 | tf_op jit(solution)/shard_map/pallas_call | solution.py:275
  33.5 23.5 %fusion.22 = (f32[2560]{0:T(1024)S(1)}, f32[2560,768]{1,0:T(8,128)S(1)}, f32[2560,768]{1,0:T(8,128)}, f32[2560,768]{1,0:T(8,128)}) fusion(f32[768]{0:T(1024)S(1)} %copy-done.24, bf16[2560,768]{1,0:T(8,128)(2,1)} %shard_map.161, bf16[768,768]{1,0:T(8,128)(2,1)} %param.14), kind=kOutput, calls=%fused_computation.93 | convolution fusion | flops 3149657600 | bytes 28718080 | tf_op jit(solution)/shard_map/dot_general | solution.py:319
  57.1 3.1 copy-done
  60.2 1.8 multiply_reduce_fusion.2
  62.7 7.3 fusion.21
  70.0 6.4 broadcast_in_dim.123.bias_ref
  76.4 53.9 %shard_map.162 = (f32[8,2560]{1,0:T(8,128)}, f32[6,5,2096,512]{3,2,1,0:T(8,128)}) custom-call(s32[1]{0:T(128)} %bitcast.count_ref, s32[1,2560]{1,0:T(1,128)} %select_n.188.lab_ref, bf16[2560,768]{1,0:T(8,128)(2,1)} %get-tuple-element.38.tok_ref, bf16[12576,768]{1,0:T(8,128)(2,1)} %embed_ref.7, f32[12576,128]{1,0:T(8,128)} %broadcast_in_dim.123.bias_ref), custom_call_target="tpu_custom_call" | custom-call | flops 24999999488 | bytes 40000000 | tf_op jit(solution)/shard_map/pallas_call | solution.py:275
  130.3 0.9 slice.30
  131.2 15.8 %all-gather.1 = f32[16,4,2560]{2,1,0:T(4,128)S(1)} all-gather(f32[1,4,2560]{2,1,0:T(4,128)S(1)} %maximum_bitcast_fusion), channel_id=2, replica_groups=mesh['dp'=4,'tp'=4] {'dp','tp'}, dimensions={0}, use_global_device_ids=true | all-gather | bytes 696320 | tf_op jit(solution)/shard_map/all_gather | solution.py:339
  147.0 1.0 fusion.25
  151.8 96.7 %shard_map.163 = (f32[12576,768]{1,0:T(8,128)}, f32[12576,128]{1,0:T(8,128)}, f32[2560,768]{1,0:T(8,128)}) custom-call(s32[1]{0:T(128)} %bitcast.count_ref, s32[1,2560]{1,0:T(1,128)} %select_n.188.lab_ref, f32[4,2560]{1,0:T(4,128)} %get-tuple-element.50.meta_ref, bf16[2560,768]{1,0:T(8,128)(2,1)} %get-tuple-element.38.tok_ref, bf16[12576,768]{1,0:T(8,128)(2,1)} %embed_ref.7, ...), custom_call_target="tpu_custom_call" | custom-call | flops 49999998976 | bytes 40000000 | tf_op jit(solution)/shard_map/pallas_call | solution.py:275
  248.6 140.6 %all-reduce.3.cloned.1.call-done = f32[2560,768]{1,0:T(8,128)} async-done(((f32[2560,768]{1,0:T(8,128)}), f32[2560,768]{1,0:T(8,128)}) %all-reduce.3.cloned.1.call-update) | async-done | bytes 7864336 | tf_op jit(solution)/shard_map/psum | solution.py:365
  389.2 7.2 fusion.19
  397.0 6.6 multiply_reduce_fusion
  404.0 8.0 %fusion.20 = (f32[768]{0:T(1024)S(1)}, bf16[2560,768]{1,0:T(8,128)(2,1)S(1)}) fusion(f32[2560,768]{1,0:T(8,128)S(1)} %bitcast.75, f32[2560]{0:T(1024)S(1)} %negate_multiply_fusion.1, f32[2560]{0:T(1024)S(1)} %multiply_multiply_fusion.6, f32[2560,768]{1,0:T(8,128)S(1)} %bitcast.73, f32[2560]{0:T(1024)S(1)} %copy-done.5, f32[2560]{0:T(1024)S(1)} %copy-done.12, ...), kind=kLoop, calls=%fused_computation.91 | loop fusion | flops 45219072 | bytes 35439616 | tf_op jit(solution)/shard_map/reduce_sum | solution.py:401
  412.1 8.3 %fusion.7 = f32[768,768]{1,0:T(8,128)} fusion(bf16[2560,768]{1,0:T(8,128)(2,1)} %shard_map.161, bf16[2560,768]{1,0:T(8,128)(2,1)S(1)} %get-tuple-element.36), kind=kOutput, calls=%fused_computation.25 | convolution fusion | flops 3019898880 | bytes 10223616 | tf_op jit(solution)/shard_map/nd,ne->de/dot_general | solution.py:400
  420.5 7.1 concatenate.11
  427.7 2.9 constant_dynamic-slice_fusion
  436.7 0.8 bitcast_dynamic-update-slice_fusion
  437.6 1.2 dynamic_update_slice.10
  442.0 8.5 %fusion.9.rows_ref = f32[2560,768]{1,0:T(8,128)} fusion(bf16[768,768]{1,0:T(8,128)(2,1)S(1)} %copy-done.26, bf16[2560,768]{1,0:T(8,128)(2,1)} %copy-done.2), kind=kOutput, calls=%fused_computation.27 | convolution fusion | flops 3019898880 | bytes 12976128 | tf_op jit(solution)/shard_map/ne,de->nd/dot_general | solution.py:405
  450.5 16.2 %shard_map.164 = bf16[32,512,768]{2,1,0:T(8,128)(2,1)} custom-call(s32[32]{0:T(128)} %get-tuple-element.44.base_ref, s32[32,1,128]{2,1,0:T(1,128)} %bitcast.82, f32[2560,768]{1,0:T(8,128)} %fusion.9.rows_ref), custom_call_target="tpu_custom_call" | custom-call | flops 8000000000 | bytes 40000000 | tf_op jit(solution)/shard_map/pallas_call | solution.py:275
  466.8 103.8 %all-reduce.5.cloned.1.call-done = f32[776,768]{1,0:T(8,128)} async-done(((f32[776,768]{1,0:T(8,128)}), f32[776,768]{1,0:T(8,128)}) %all-reduce.5.cloned.1.call-update) | async-done | bytes 2383888 | tf_op jit(solution)/shard_map/psum | solution.py:403
  570.5 3.2 slice.44
  573.7 1.5 slice_reduce_fusion.1
  575.2 130.2 %shard_map.165 = (f32[12576,768]{1,0:T(8,128)}, f32[12576,128]{1,0:T(8,128)}) custom-call(s32[3]{0:T(128)} %pad_add_fusion.plan_ref, s32[30]{0:T(128)} %compare_select_fusion.6.src_ref, s32[30]{0:T(128)} %compare_select_fusion.5.dst_ref, s32[1,7936]{1,0:T(1,128)} %slice_convert_fusion.lab_ref, ...), custom_call_target="tpu_custom_call", output_to_operand_aliasing={{0}: (7, {}), {1}: (8, {})} | custom-call | flops 99999997952 | bytes 40000000 | tf_op jit(solution)/shard_map/pallas_call | solution.py:275
  705.4 73.6 %shard_map.166 = (f32[12576,768]{1,0:T(8,128)}, f32[12576,128]{1,0:T(8,128)}) custom-call(s32[3]{0:T(128)} %pad_add_fusion.plan_ref, s32[30]{0:T(128)} %compare_select_fusion.6.src_ref, s32[30]{0:T(128)} %compare_select_fusion.5.dst_ref, s32[1,7936]{1,0:T(1,128)} %slice_convert_fusion.lab_ref, ...), custom_call_target="tpu_custom_call", output_to_operand_aliasing={{0}: (7, {}), {1}: (8, {})} | custom-call | flops 49999998976 | bytes 40000000 | tf_op jit(solution)/shard_map/pallas_call | solution.py:275
  779.0 5.1 reduce_sum.198
  (110 shorter events, 12.2 us)
Async XLA Ops:
  8.0 381.2 %all-reduce.3.cloned.1.call-start = ((), (), s32[]{:S(2)}) async-start(), calls=%async_computation | async-start | bytes 15728640 | tf_op jit(solution)/shard_map/psum | solution.py:365
  18.1 15.4 %copy-start.24 = (f32[768]{0:T(1024)S(1)}, f32[768]{0:T(1024)}, u32[]{:S(2)}) copy-start(f32[768]{0:T(1024)} %param.15) | copy-start | bytes 9220
  57.1 3.1 copy-start
  57.1 5.6 copy-start.19
  57.1 5.6 copy-start.23
  57.1 12.9 %copy-start.4 = (f32[2560]{0:T(1024)}, f32[2560]{0:T(1024)S(1)}, u32[]{:S(2)}) copy-start(f32[2560]{0:T(1024)S(1)} %broadcast_multiply_fusion) | copy-start | bytes 30724
  62.7 7.4 copy-start.11
  62.7 7.3 copy-start.21
  149.0 2.8 copy-start.8
  150.0 1.8 copy-start.6
  248.5 140.7 %copy-start.5 = (f32[2560]{0:T(1024)S(1)}, f32[2560]{0:T(1024)}, u32[]{:S(2)}) copy-start(f32[2560]{0:T(1024)} %copy-done.4) | copy-start | bytes 30724
  248.5 140.7 %copy-start.20 = (f32[768]{0:T(1024)S(1)}, f32[768]{0:T(1024)}, u32[]{:S(2)}) copy-start(f32[768]{0:T(1024)} %param.16) | copy-start | bytes 9220
  248.5 147.9 %copy-start.18 = (f32[2560]{0:T(1024)S(1)}, f32[2560]{0:T(1024)}, u32[]{:S(2)}) copy-start(f32[2560]{0:T(1024)} %copy-done.17) | copy-start | bytes 30724
  248.6 147.9 %copy-start.12 = (f32[2560]{0:T(1024)S(1)}, f32[2560]{0:T(1024)}, u32[]{:S(2)}) copy-start(f32[2560]{0:T(1024)} %copy-done.11) | copy-start | bytes 30724
  248.6 322.0 %all-reduce.5.cloned.1.call-start = ((), (), s32[]{:S(2)}) async-start(), calls=%async_computation.1 | async-start | bytes 4767744 | tf_op jit(solution)/shard_map/psum | solution.py:403
  389.2 7.8 copy-start.1
  389.2 14.4 %slice-start = ((s8[7864320]{0:T(1024)(128)(4,1)}), s8[4194304]{0:T(1024)(128)(4,1)S(1)}, s32[]{:S(2)}) async-start(s8[7864320]{0:T(1024)(128)(4,1)} %bitcast.72), calls=%async_computation.3 | async-start | bytes 8388608
  389.2 14.4 %slice-start.2 = ((s8[7864320]{0:T(1024)(128)(4,1)}), s8[4194304]{0:T(1024)(128)(4,1)S(1)}, s32[]{:S(2)}) async-start(s8[7864320]{0:T(1024)(128)(4,1)} %bitcast.74), calls=%async_computation.5 | async-start | bytes 8388608
  397.0 6.6 slice-start.1
  397.0 7.0 slice-start.3
  397.0 7.0 copy-start.25
  412.0 8.3 %copy-start.2 = (bf16[2560,768]{1,0:T(8,128)(2,1)}, bf16[2560,768]{1,0:T(8,128)(2,1)S(1)}, u32[]{:S(2)}) copy-start(bf16[2560,768]{1,0:T(8,128)(2,1)S(1)} %get-tuple-element.36) | copy-start | bytes 11796484
  420.3 10.3 %copy-start.22 = (s32[4]{0:T(128)S(1)}, s32[4]{0:T(128)}, u32[]{:S(2)}) copy-start(s32[4]{0:T(128)} %get-tuple-element.33) | copy-start | bytes 52
  420.3 14.9 %copy-start.7 = (f32[4,2560]{1,0:T(4,128)S(1)}, f32[4,2560]{1,0:T(4,128)}, u32[]{:S(2)}) copy-start(f32[4,2560]{1,0:T(4,128)} %copy-done.6) | copy-start | bytes 122884
  420.3 14.9 %copy-start.9 = (pred[4,1,1,2560]{3,0,2,1:T(4,128)(4,1)S(1)}, pred[4,1,1,2560]{3,0,2,1:T(4,128)(4,1)}, u32[]{:S(2)}) copy-start(pred[4,1,1,2560]{3,0,2,1:T(4,128)(4,1)} %copy-done.8) | copy-start | bytes 30724
  420.3 14.9 %copy-start.13 = (f32[4,2560]{1,0:T(4,128)S(1)}, f32[4,2560]{1,0:T(4,128)}, u32[]{:S(2)}) copy-start(f32[4,2560]{1,0:T(4,128)} %get-tuple-element.46) | copy-start | bytes 122884
  420.3 16.3 %copy-start.16 = (f32[4,7936]{1,0:T(4,128)S(1)}, f32[4,7936]{1,0:T(4,128)}, u32[]{:S(2)}) copy-start(f32[4,7936]{1,0:T(4,128)} %constant.245.clone.1) | copy-start | bytes 380932
  420.4 17.2 %copy-start.15 = (f32[4,2560]{1,0:T(4,128)S(1)}, f32[4,2560]{1,0:T(4,128)}, u32[]{:S(2)}) copy-start(f32[4,2560]{1,0:T(4,128)} %get-tuple-element.49) | copy-start | bytes 122884
  420.4 18.4 %copy-start.14 = (f32[4,2560]{1,0:T(4,128)S(1)}, f32[4,2560]{1,0:T(4,128)}, u32[]{:S(2)}) copy-start(f32[4,2560]{1,0:T(4,128)} %get-tuple-element.48) | copy-start | bytes 122884
  420.4 21.6 %copy-start.26 = (bf16[768,768]{1,0:T(8,128)(2,1)S(1)}, bf16[768,768]{1,0:T(8,128)(2,1)}, u32[]{:S(2)}) copy-start(bf16[768,768]{1,0:T(8,128)(2,1)} %param.14) | copy-start | bytes 3538948
  427.6 147.6 %all-gather.4.cloned.1.call-start = ((), (), s32[]{:S(2)}) async-start(), calls=%async_computation.2 | async-start | bytes 33423360 | tf_op jit(solution)/shard_map/all_gather | solution.py:324
  439.5 1.8 copy-start.10
  (2 other events, 1.3 us)
Sparse Core Ops, SparseCore 0:
  248.7 140.4 all-reduce.2
  427.7 142.7 all-reduce.4
Sparse Core Ops, SparseCore 1:
  430.7 130.7 all-gather.3

commit v4 on v3

--- a/solution.py
+++ b/solution.py
@@ -1,4 +1,5 @@
 import functools
+import math
 
 import jax
 import jax.numpy as jnp
@@ -10,6 +11,8 @@
 
 LN_EPS = 1e-12
 LOSS_EPS = 1e-5
+SQRT_HALF = 0.5 ** 0.5
+BELL_PEAK = (2.0 * math.pi) ** -0.5
 VOCAB_BLOCKS = 6
 TOK = 256
 CHUNK = 256
@@ -21,12 +24,12 @@
 VMEM_LIMIT = 67_000_000
 
 
-def gelu_norm(pre_act, gamma, beta):
-    activated = jax.nn.gelu(pre_act, approximate=False)
-    mean_val = jnp.mean(activated, axis=-1, keepdims=True)
-    centered = activated - mean_val
-    variance = jnp.mean(centered * centered, axis=-1, keepdims=True)
-    return centered * lax.rsqrt(variance + LN_EPS) * gamma + beta
+def normalize(pre_act):
+    bell = 0.5 * (1.0 + lax.erf(pre_act * SQRT_HALF))
+    activated = pre_act * bell
+    centered = activated - jnp.mean(activated, axis=-1, keepdims=True)
+    scale = lax.rsqrt(jnp.mean(centered * centered, axis=-1, keepdims=True) + LN_EPS)
+    return centered * scale, scale, bell
 
 
 def dot_nt(a, b):
@@ -46,30 +49,74 @@
     return jnp.where(ids == row[:, :PICK], 1.0, 0.0).astype(jnp.bfloat16)
 
 
-def pick_kernel(base_ref, idx_ref, hidden_ref, out_ref, acc):
+def pick_kernel(base_ref, count_ref, idx_ref, hidden_ref, weight_ref, vecs_ref, picked_ref, normed_ref, tok_ref, acc):
     step = pl.program_id(0)
+    picks = base_ref.shape[0] // SEQS
+    block = step - picks
 
     @pl.when(step == 0)
     def _():
         acc[...] = jnp.zeros_like(acc)
 
-    picked = [dot_tn(hot_rows(idx_ref[k], hidden_ref.shape[1]), hidden_ref[k]) for k in range(SEQS)]
-    for k, rows in enumerate(picked):
-        base = pl.multiple_of(base_ref[step * SEQS + k], 8)
-        acc[pl.ds(base, 16), :] += rows[:16]
-        acc[pl.ds(base + 16, PICK - 16), :] = rows[16:]
-
-    @pl.when(step == pl.num_programs(0) - 1)
-    def _():
-        out_ref[...] = acc[...].astype(jnp.bfloat16)
-
-
-def place_kernel(base_ref, idx_ref, rows_ref, out_ref):
+    @pl.when(step < picks)
+    def _():
+        picked = [dot_tn(hot_rows(idx_ref[k], hidden_ref.shape[1]), hidden_ref[k]) for k in range(SEQS)]
+        for k, rows in enumerate(picked):
+            base = pl.multiple_of(base_ref[step * SEQS + k], 8)
+            acc[pl.ds(base, 16), :] += rows[:16]
+            acc[pl.ds(base + 16, PICK - 16), :] = rows[16:]
+
+    @pl.when(step >= picks)
+    def _():
+        rows = acc[pl.ds(pl.multiple_of(block * TOK, TOK), TOK), :].astype(jnp.bfloat16)
+        picked_ref[...] = rows
+
+        @pl.when(block * TOK < count_ref[0])
+        def _():
+            unit, _, _ = normalize(dot_nn(rows, weight_ref[...]) + vecs_ref[0:1, :])
+            normed = unit * vecs_ref[1:2, :] + vecs_ref[2:3, :]
+            normed_ref[...] = normed
+            tok_ref[...] = normed.astype(jnp.bfloat16)
+
+        @pl.when(block * TOK >= count_ref[0])
+        def _():
+            normed_ref[...] = jnp.zeros_like(normed_ref)
+            tok_ref[...] = jnp.zeros_like(tok_ref)
+
+
+def back_kernel(base_ref, count_ref, idx_ref, dnormed_ref, picked_ref, weight_ref, vecs_ref, sums_ref, dhidden_ref, drows):
     step = pl.program_id(0)
-    for k in range(SEQS):
-        base = pl.multiple_of(base_ref[step * SEQS + k], 8)
-        rows = rows_ref[pl.ds(base, PICK), :].astype(jnp.bfloat16)
-        out_ref[k] = dot_nn(hot_rows(idx_ref[k], out_ref.shape[1]), rows).astype(jnp.bfloat16)
+    blocks = drows.shape[0] // TOK
+    width = weight_ref.shape[0]
+
+    @pl.when(step == 0)
+    def _():
+        sums_ref[...] = jnp.zeros_like(sums_ref)
+        drows[...] = jnp.zeros_like(drows)
+
+    @pl.when((step < blocks) & (step * TOK < count_ref[0]))
+    def _():
+        pre_act = dot_nn(picked_ref[...], weight_ref[...]) + vecs_ref[0:1, :]
+        unit, scale, bell = normalize(pre_act)
+        dnormed = dnormed_ref[...]
+        dunit = dnormed * vecs_ref[1:2, :]
+        dcentered = scale * (dunit - unit * jnp.mean(dunit * unit, axis=-1, keepdims=True))
+        dactivated = dcentered - jnp.mean(dcentered, axis=-1, keepdims=True)
+        slope = bell + pre_act * (BELL_PEAK * jnp.exp(-0.5 * pre_act * pre_act))
+        dpre = dactivated * slope
+        dpre_bf = dpre.astype(jnp.bfloat16)
+        sums_ref[:width, :] += dot_tn(picked_ref[...], dpre_bf)
+        sums_ref[width:width + 1, :] += jnp.sum(dpre, axis=0, keepdims=True)
+        sums_ref[width + 1:width + 2, :] += jnp.sum(dnormed * unit, axis=0, keepdims=True)
+        sums_ref[width + 2:width + 3, :] += jnp.sum(dnormed, axis=0, keepdims=True)
+        drows[pl.ds(pl.multiple_of(step * TOK, TOK), TOK), :] = dot_nt(dpre_bf, weight_ref[...])
+
+    @pl.when(step >= blocks)
+    def _():
+        for k in range(SEQS):
+            base = pl.multiple_of(base_ref[(step - blocks) * SEQS + k], 8)
+            rows = drows[pl.ds(base, PICK), :].astype(jnp.bfloat16)
+            dhidden_ref[k] = dot_nn(hot_rows(idx_ref[k], dhidden_ref.shape[1]), rows).astype(jnp.bfloat16)
 
 
 def for_blocks(count, body):
@@ -311,14 +358,16 @@
         count = jnp.sum(live)
         blocks = ((count + TOK - 1) // TOK).reshape(1)
 
-        picked = run(
-            pick_kernel, (base,), batch // SEQS, (idx_rows, hidden),
-            [by_rows((SEQS, 1, 128)), by_rows((SEQS, seq_len, width))], whole((rows, width)),
-            jax.ShapeDtypeStruct((rows, width), bf16), [pltpu.VMEM((rows, width), f32)], 8_000_000_000,
+        picks, row_blocks = batch // SEQS, rows // TOK
+        vecs = jnp.stack([b_t, gamma, beta] + [jnp.zeros_like(b_t)] * 5)
+        early = lambda shape: pl.BlockSpec(shape, lambda step, *_: (jnp.minimum(step, picks - 1),) + (0,) * (len(shape) - 1))
+        late = pl.BlockSpec((TOK, width), lambda step, *_: (jnp.maximum(step - picks, 0), 0))
+        picked, normed, tok = run(
+            pick_kernel, (base, count.reshape(1)), picks + row_blocks, (idx_rows, hidden, w_t, vecs),
+            [early((SEQS, 1, 128)), early((SEQS, seq_len, width)), whole((width, width)), whole((8, width))], [late] * 3,
+            [jax.ShapeDtypeStruct((rows, width), bf16), jax.ShapeDtypeStruct((rows, width), f32), jax.ShapeDtypeStruct((rows, width), bf16)],
+            [pltpu.VMEM((rows, width), f32)], 8_000_000_000,
         )
-        pre_act = jnp.dot(picked, w_t, preferred_element_type=f32) + b_t
-        normed, norm_vjp = jax.vjp(gelu_norm, pre_act, gamma, beta)
-        tok = normed.astype(bf16)
         share = rows // shards
         mine = lax.dynamic_slice(normed, (me_tp * share, 0), (share, width))
         tok_all = lax.all_gather(mine, ("dp", "tp"), tiled=True)
@@ -395,19 +444,17 @@
             )
         d_out_bias = jnp.sum(d_bias, axis=1)
 
-        d_pre, d_gamma, d_beta = norm_vjp(d_normed)
-        d_pre_bf = d_pre.astype(bf16)
-        d_w_t = jnp.einsum("nd,ne->de", picked, d_pre_bf, preferred_element_type=f32)
-        d_b_t = jnp.sum(d_pre, axis=0)
-        small = jnp.stack([d_b_t, d_gamma, d_beta] + [jnp.zeros_like(d_b_t)] * 5)
-        sums = lax.psum(jnp.concatenate([d_w_t, small], axis=0), "dp")
+        first_rows = pl.BlockSpec((TOK, width), lambda step, *_: (jnp.minimum(step, row_blocks - 1), 0))
+        then_seqs = lambda shape: pl.BlockSpec(shape, lambda step, *_: (jnp.maximum(step - row_blocks, 0),) + (0,) * (len(shape) - 1))
+        sums, d_hidden = run(
+            back_kernel, (base, count.reshape(1)), row_blocks + picks, (idx_rows, d_normed, picked, w_t, vecs),
+            [then_seqs((SEQS, 1, 128)), first_rows, first_rows, whole((width, width)), whole((8, width))],
+            [whole((width + 8, width)), then_seqs((SEQS, seq_len, width))],
+            [jax.ShapeDtypeStruct((width + 8, width), f32), jax.ShapeDtypeStruct((batch, seq_len, width), bf16)],
+            [pltpu.VMEM((rows, width), f32)], 8_000_000_000,
+        )
+        sums = lax.psum(sums, "dp")
         d_w_t, d_b_t, d_gamma, d_beta = sums[:width], sums[width], sums[width + 1], sums[width + 2]
-        d_rows = jnp.einsum("ne,de->nd", d_pre_bf, w_t, preferred_element_type=f32)
-        d_hidden = run(
-            place_kernel, (base,), batch // SEQS, (idx_rows, d_rows),
-            [by_rows((SEQS, 1, 128)), whole((rows, width))], by_rows((SEQS, seq_len, width)),
-            jax.ShapeDtypeStruct((batch, seq_len, width), bf16), [], 8_000_000_000,
-        )
         return loss, d_hidden, d_w_t, d_b_t, d_gamma, d_beta, d_embed, d_out_bias
 
     in_specs = (P("dp", None, None), P("dp", None), P("dp", None), P("dp", None), P(None, None), P(None), P(None), P(None), P("tp", None), P("tp"))

time: 806 us -> 777 us (0.964)
  the two profiles are of different devices: /device:TPU:0 before, /device:TPU:4 now
where the time goes in v4:
time: 777 us; the launch traced here: 768 us
  Pallas kernels  401 us (52%)
  waiting for transfers between devices  284 us (37%)
  between operations  23.3 us (3%)
  local copies, waits for them, and re-layouts  22.9 us (3%)
  blocking collectives  18.8 us (2%)
  other arithmetic  18.7 us (2%)
    pallas_call x6, Pallas kernels, run(): pl.pallas_call(kernel, grid_spec=pltpu.PrefetchScalarGridSpec(num_scalar_...  401 us
    psum x1, waiting for transfers between devices, local_step(): d_normed = lax.psum(d_tok, 'tp')  154 us
    psum x1, waiting for transfers between devices, local_step(): sums = lax.psum(sums, 'dp')  130 us
    all_gather x1, blocking collectives, local_step(): lax.all_gather(packet, ('dp', 'tp')).reshape(groups, shards, 4, rows)  18.8 us
  transfers between devices with their start and end apart: 3, of which 2 were waited for; matrix products, arithmetic and copies ran while one was open for 2% of the time, Pallas kernels for 0%

profile of v4, /device:TPU:4, one launch (start us, length us, event | category | flops | bytes accessed | tf_op | source)
XLA Modules:
  0.0 768.3 jit_solution(11909545391547303796)
XLA Ops:
  8.0 0.8 reduce_sum.101
  9.0 1.2 fusion.7
  10.8 0.7 broadcast_add_fusion.2
  11.8 2.9 select_reduce_fusion
  15.3 0.7 broadcast_add_fusion.1
  16.0 1.0 select_reduce_fusion.1
  17.6 0.7 stack.34
  18.3 0.7 stack.35
  19.0 0.7 stack.36
  20.3 23.1 %shard_map.161 = (bf16[2560,768]{1,0:T(8,128)(2,1)}, f32[2560,768]{1,0:T(8,128)}, bf16[2560,768]{1,0:T(8,128)(2,1)}) custom-call(s32[32]{0:T(128)} %get-tuple-element.43.base_ref, s32[1]{0:T(128)} %bitcast.1.count_ref, s32[32,1,128]{2,1,0:T(1,128)} %bitcast.72, bf16[32,512,768]{2,1,0:T(8,128)(2,1)} %hidden_ref.1, bf16[768,768]{1,0:T(8,128)(2,1)} %weight_ref.3, ...), custom_call_target="tpu_custom_call" | custom-call | flops 8000000000 | bytes 40000000 | tf_op jit(solution)/shard_map/pallas_call | solution.py:322
  43.4 6.4 broadcast_in_dim.112.bias_ref
  49.9 48.6 %shard_map.162 = (f32[8,2560]{1,0:T(8,128)}, f32[6,5,2096,512]{3,2,1,0:T(8,128)}) custom-call(s32[1]{0:T(128)} %bitcast.count_ref, s32[1,2560]{1,0:T(1,128)} %select_n.188.lab_ref, bf16[2560,768]{1,0:T(8,128)(2,1)} %get-tuple-element.22.tok_ref, bf16[12576,768]{1,0:T(8,128)(2,1)} %embed_ref.7, f32[12576,128]{1,0:T(8,128)} %broadcast_in_dim.112.bias_ref), custom_call_target="tpu_custom_call" | custom-call | flops 24999999488 | bytes 40000000 | tf_op jit(solution)/shard_map/pallas_call | solution.py:322
  98.4 0.9 slice.30
  99.4 18.8 %all-gather.1 = f32[16,4,2560]{2,1,0:T(4,128)S(1)} all-gather(f32[1,4,2560]{2,1,0:T(4,128)S(1)} %maximum_bitcast_fusion), channel_id=2, replica_groups=mesh['dp'=4,'tp'=4] {'dp','tp'}, dimensions={0}, use_global_device_ids=true | all-gather | bytes 696320 | tf_op jit(solution)/shard_map/all_gather | solution.py:388
  118.2 1.0 fusion.8
  119.5 0.7 convert_reduce_fusion
  121.6 0.7 copy-done
  122.3 0.7 dynamic-slice_bitcast_fusion
  122.9 84.8 %shard_map.163 = (f32[12576,768]{1,0:T(8,128)}, f32[12576,128]{1,0:T(8,128)}, f32[2560,768]{1,0:T(8,128)}) custom-call(s32[1]{0:T(128)} %bitcast.count_ref, s32[1,2560]{1,0:T(1,128)} %select_n.188.lab_ref, f32[4,2560]{1,0:T(4,128)} %get-tuple-element.49.meta_ref, bf16[2560,768]{1,0:T(8,128)(2,1)} %get-tuple-element.22.tok_ref, bf16[12576,768]{1,0:T(8,128)(2,1)} %embed_ref.7, ...), custom_call_target="tpu_custom_call" | custom-call | flops 49999998976 | bytes 40000000 | tf_op jit(solution)/shard_map/pallas_call | solution.py:322
  207.9 153.6 %all-reduce.3.cloned.1.call-done.dnormed_ref = f32[2560,768]{1,0:T(8,128)} async-done(((f32[2560,768]{1,0:T(8,128)}), f32[2560,768]{1,0:T(8,128)}) %all-reduce.3.cloned.1.call-update) | async-done | bytes 7864336 | tf_op jit(solution)/shard_map/psum | solution.py:414
  361.5 29.6 %shard_map.164 = (f32[776,768]{1,0:T(8,128)}, bf16[32,512,768]{2,1,0:T(8,128)(2,1)}) custom-call(s32[32]{0:T(128)} %get-tuple-element.43.base_ref, s32[1]{0:T(128)} %bitcast.1.count_ref, s32[32,1,128]{2,1,0:T(1,128)} %bitcast.73, f32[2560,768]{1,0:T(8,128)} %all-reduce.3.cloned.1.call-done.dnormed_ref, bf16[2560,768]{1,0:T(8,128)(2,1)} %get-tuple-element.26.picked_ref, ...), custom_call_target="tpu_custom_call" | custom-call | flops 8000000000 | bytes 40000000 | tf_op jit(solution)/shard_map/pallas_call | solution.py:322
  391.2 3.0 constant_dynamic-slice_fusion
  400.4 0.8 bitcast_dynamic-update-slice_fusion
  401.2 0.7 dynamic_update_slice.10
  401.9 0.7 dynamic_update_slice.11.meta_ref
  404.4 0.6 slice_convert_fusion.lab_ref
  405.0 129.9 %all-reduce.5.cloned.1.call-done = f32[776,768]{1,0:T(8,128)} async-done(((f32[776,768]{1,0:T(8,128)}), f32[776,768]{1,0:T(8,128)}) %all-reduce.5.cloned.1.call-update) | async-done | bytes 2383888 | tf_op jit(solution)/shard_map/psum | solution.py:456
  534.9 3.2 slice.44
  538.1 1.5 slice_reduce_fusion.1
  539.6 137.2 %shard_map.165 = (f32[12576,768]{1,0:T(8,128)}, f32[12576,128]{1,0:T(8,128)}) custom-call(s32[3]{0:T(128)} %pad_add_fusion.plan_ref, s32[30]{0:T(128)} %compare_select_fusion.6.src_ref, s32[30]{0:T(128)} %compare_select_fusion.5.dst_ref, s32[1,7936]{1,0:T(1,128)} %slice_convert_fusion.lab_ref, ...), custom_call_target="tpu_custom_call", output_to_operand_aliasing={{0}: (7, {}), {1}: (8, {})} | custom-call | flops 99999997952 | bytes 40000000 | tf_op jit(solution)/shard_map/pallas_call | solution.py:322
  676.9 77.5 %shard_map.166 = (f32[12576,768]{1,0:T(8,128)}, f32[12576,128]{1,0:T(8,128)}) custom-call(s32[3]{0:T(128)} %pad_add_fusion.plan_ref, s32[30]{0:T(128)} %compare_select_fusion.6.src_ref, s32[30]{0:T(128)} %compare_select_fusion.5.dst_ref, s32[1,7936]{1,0:T(1,128)} %slice_convert_fusion.lab_ref, ...), custom_call_target="tpu_custom_call", output_to_operand_aliasing={{0}: (7, {}), {1}: (8, {})} | custom-call | flops 49999998976 | bytes 40000000 | tf_op jit(solution)/shard_map/pallas_call | solution.py:322
  754.4 5.1 reduce_sum.112
  (56 shorter events, 6.4 us)
Async XLA Ops:
  8.0 353.5 %all-reduce.3.cloned.1.call-start = ((), (), s32[]{:S(2)}) async-start(), calls=%async_computation | async-start | bytes 15728640 | tf_op jit(solution)/shard_map/psum | solution.py:414
  120.1 2.8 copy-start.3
  121.2 1.8 copy-start.1
  121.6 0.7 copy-start
  207.7 327.2 %all-reduce.5.cloned.1.call-start = ((), (), s32[]{:S(2)}) async-start(), calls=%async_computation.1 | async-start | bytes 4767744 | tf_op jit(solution)/shard_map/psum | solution.py:456
  391.1 3.2 copy-start.10
  391.1 7.8 %copy-start.2 = (f32[4,2560]{1,0:T(4,128)S(1)}, f32[4,2560]{1,0:T(4,128)}, u32[]{:S(2)}) copy-start(f32[4,2560]{1,0:T(4,128)} %copy-done.1) | copy-start | bytes 122884
  391.1 7.8 %copy-start.4 = (pred[4,1,1,2560]{3,0,2,1:T(4,128)(4,1)S(1)}, pred[4,1,1,2560]{3,0,2,1:T(4,128)(4,1)}, u32[]{:S(2)}) copy-start(pred[4,1,1,2560]{3,0,2,1:T(4,128)(4,1)} %copy-done.3) | copy-start | bytes 30724
  391.1 7.8 %copy-start.6 = (f32[4,2560]{1,0:T(4,128)S(1)}, f32[4,2560]{1,0:T(4,128)}, u32[]{:S(2)}) copy-start(f32[4,2560]{1,0:T(4,128)} %get-tuple-element.45) | copy-start | bytes 122884
  391.1 9.2 %copy-start.9 = (f32[4,7936]{1,0:T(4,128)S(1)}, f32[4,7936]{1,0:T(4,128)}, u32[]{:S(2)}) copy-start(f32[4,7936]{1,0:T(4,128)} %constant.175.clone.1) | copy-start | bytes 380932
  391.1 10.1 %copy-start.8 = (f32[4,2560]{1,0:T(4,128)S(1)}, f32[4,2560]{1,0:T(4,128)}, u32[]{:S(2)}) copy-start(f32[4,2560]{1,0:T(4,128)} %get-tuple-element.48) | copy-start | bytes 122884
  391.1 10.8 %copy-start.7 = (f32[4,2560]{1,0:T(4,128)S(1)}, f32[4,2560]{1,0:T(4,128)}, u32[]{:S(2)}) copy-start(f32[4,2560]{1,0:T(4,128)} %get-tuple-element.47) | copy-start | bytes 122884
  391.2 148.4 %all-gather.4.cloned.1.call-start = ((), (), s32[]{:S(2)}) async-start(), calls=%async_computation.2 | async-start | bytes 33423360 | tf_op jit(solution)/shard_map/all_gather | solution.py:373
  402.7 1.7 copy-start.5
Sparse Core Ops, SparseCore 0:
  207.8 153.6 all-reduce.2
  391.3 143.5 all-reduce.4
Sparse Core Ops, SparseCore 1:
  394.3 131.4 all-gather.3

commit v5 on v4

--- a/solution.py
+++ b/solution.py
@@ -132,8 +132,8 @@
 
 
 def strips(height):
-    size = (height // 4 + 15) // 16 * 16
-    return [(at, min(size, height - at)) for at in range(0, height, size)]
+    size = height // 4 // 256 * 256
+    return [(k * size, size if k < 3 else height - 3 * size) for k in range(4)]
 
 
 def tile_bias(bias_ref, at, size, width):
@@ -167,9 +167,15 @@
         lab = lab_ref[0:1, cols] - vblk * height
         parts = []
         target = jnp.zeros((1, width), jnp.float32)
-        for at, size in strips(height):
+        todo = strips(height)
+
+        def logits(at, size):
             z_ref[slot, at:at + size, :width] = dot_nt(embed_ref[at:at + size, :], tok) + tile_bias(bias_ref, at, size, width)
-        for at, size in strips(height):
+
+        logits(*todo[0])
+        for k, (at, size) in enumerate(todo):
+            if k + 1 < len(todo):
+                logits(*todo[k + 1])
             z = z_ref[slot, at:at + size, :width]
             top = jnp.max(z, axis=0, keepdims=True)
             total = jnp.sum(jnp.exp(z - top), axis=0, keepdims=True)
@@ -250,7 +256,7 @@
                 grad(*todo[k + 1])
             dz = dz_ref[at:at + size, :width]
             dembed_ref[at:at + size, :] = dot_nn(dz, tok) + jnp.where(fresh, 0.0, dembed_ref[at:at + size, :])
-        dtok_ref[cols, :] += dot_tn(dz_ref[:, :width], embed_ref[...])
+            dtok_ref[cols, :] += dot_tn(dz, embed_ref[at:at + size, :])
 
     for_blocks(count_ref[0], body)
 

time: 777 us -> 770 us (level)
  no operation moved by 1% of the time
where the time goes in v5:
time: 770 us; the launch traced here: 762 us
  Pallas kernels  395 us (51%)
  waiting for transfers between devices  283 us (37%)
  between operations  23.3 us (3%)
  local copies, waits for them, and re-layouts  22.9 us (3%)
  blocking collectives  18.8 us (2%)
  other arithmetic  18.7 us (2%)
    pallas_call x6, Pallas kernels, run(): pl.pallas_call(kernel, grid_spec=pltpu.PrefetchScalarGridSpec(num_scalar_...  395 us
    psum x1, waiting for transfers between devices, local_step(): d_normed = lax.psum(d_tok, 'tp')  153 us
    psum x1, waiting for transfers between devices, local_step(): sums = lax.psum(sums, 'dp')  130 us
    all_gather x1, blocking collectives, local_step(): lax.all_gather(packet, ('dp', 'tp')).reshape(groups, shards, 4, rows)  18.8 us
  transfers between devices with their start and end apart: 3, of which 2 were waited for; matrix products, arithmetic and copies ran while one was open for 2% of the time, Pallas kernels for 0%

profile of v5, /device:TPU:4, one launch (start us, length us, event | category | flops | bytes accessed | tf_op | source)
XLA Modules:
  0.0 761.7 jit_solution(1173876148349432900)
XLA Ops:
  8.0 0.8 reduce_sum.101
  9.0 1.2 fusion.7
  10.8 0.7 broadcast_add_fusion.2
  11.8 2.9 select_reduce_fusion
  15.3 0.7 broadcast_add_fusion.1
  16.0 1.0 select_reduce_fusion.1
  17.6 0.7 stack.34
  18.3 0.7 stack.35
  19.0 0.7 stack.36
  20.3 23.1 %shard_map.161 = (bf16[2560,768]{1,0:T(8,128)(2,1)}, f32[2560,768]{1,0:T(8,128)}, bf16[2560,768]{1,0:T(8,128)(2,1)}) custom-call(s32[32]{0:T(128)} %get-tuple-element.43.base_ref, s32[1]{0:T(128)} %bitcast.1.count_ref, s32[32,1,128]{2,1,0:T(1,128)} %bitcast.72, bf16[32,512,768]{2,1,0:T(8,128)(2,1)} %hidden_ref.1, bf16[768,768]{1,0:T(8,128)(2,1)} %weight_ref.3, ...), custom_call_target="tpu_custom_call" | custom-call | flops 8000000000 | bytes 40000000 | tf_op jit(solution)/shard_map/pallas_call | solution.py:328
  43.4 6.4 broadcast_in_dim.112.bias_ref
  49.9 48.3 %shard_map.162 = (f32[8,2560]{1,0:T(8,128)}, f32[6,5,2096,512]{3,2,1,0:T(8,128)}) custom-call(s32[1]{0:T(128)} %bitcast.count_ref, s32[1,2560]{1,0:T(1,128)} %select_n.188.lab_ref, bf16[2560,768]{1,0:T(8,128)(2,1)} %get-tuple-element.22.tok_ref, bf16[12576,768]{1,0:T(8,128)(2,1)} %embed_ref.7, f32[12576,128]{1,0:T(8,128)} %broadcast_in_dim.112.bias_ref), custom_call_target="tpu_custom_call" | custom-call | flops 24999999488 | bytes 40000000 | tf_op jit(solution)/shard_map/pallas_call | solution.py:328
  98.2 0.9 slice.30
  99.1 18.8 %all-gather.1 = f32[16,4,2560]{2,1,0:T(4,128)S(1)} all-gather(f32[1,4,2560]{2,1,0:T(4,128)S(1)} %maximum_bitcast_fusion), channel_id=2, replica_groups=mesh['dp'=4,'tp'=4] {'dp','tp'}, dimensions={0}, use_global_device_ids=true | all-gather | bytes 696320 | tf_op jit(solution)/shard_map/all_gather | solution.py:394
  117.9 1.0 fusion.8
  119.1 0.7 convert_reduce_fusion
  121.3 0.7 copy-done
  121.9 0.7 dynamic-slice_bitcast_fusion
  122.6 79.1 %shard_map.163 = (f32[12576,768]{1,0:T(8,128)}, f32[12576,128]{1,0:T(8,128)}, f32[2560,768]{1,0:T(8,128)}) custom-call(s32[1]{0:T(128)} %bitcast.count_ref, s32[1,2560]{1,0:T(1,128)} %select_n.188.lab_ref, f32[4,2560]{1,0:T(4,128)} %get-tuple-element.49.meta_ref, bf16[2560,768]{1,0:T(8,128)(2,1)} %get-tuple-element.22.tok_ref, bf16[12576,768]{1,0:T(8,128)(2,1)} %embed_ref.7, ...), custom_call_target="tpu_custom_call" | custom-call | flops 49999998976 | bytes 40000000 | tf_op jit(solution)/shard_map/pallas_call | solution.py:328
  201.9 152.9 %all-reduce.3.cloned.1.call-done.dnormed_ref = f32[2560,768]{1,0:T(8,128)} async-done(((f32[2560,768]{1,0:T(8,128)}), f32[2560,768]{1,0:T(8,128)}) %all-reduce.3.cloned.1.call-update) | async-done | bytes 7864336 | tf_op jit(solution)/shard_map/psum | solution.py:420
  354.9 29.6 %shard_map.164 = (f32[776,768]{1,0:T(8,128)}, bf16[32,512,768]{2,1,0:T(8,128)(2,1)}) custom-call(s32[32]{0:T(128)} %get-tuple-element.43.base_ref, s32[1]{0:T(128)} %bitcast.1.count_ref, s32[32,1,128]{2,1,0:T(1,128)} %bitcast.73, f32[2560,768]{1,0:T(8,128)} %all-reduce.3.cloned.1.call-done.dnormed_ref, bf16[2560,768]{1,0:T(8,128)(2,1)} %get-tuple-element.26.picked_ref, ...), custom_call_target="tpu_custom_call" | custom-call | flops 8000000000 | bytes 40000000 | tf_op jit(solution)/shard_map/pallas_call | solution.py:328
  384.6 3.0 constant_dynamic-slice_fusion
  393.8 0.8 bitcast_dynamic-update-slice_fusion
  394.6 0.7 dynamic_update_slice.10
  395.3 0.7 dynamic_update_slice.11.meta_ref
  397.7 0.6 slice_convert_fusion.lab_ref
  398.4 129.9 %all-reduce.5.cloned.1.call-done = f32[776,768]{1,0:T(8,128)} async-done(((f32[776,768]{1,0:T(8,128)}), f32[776,768]{1,0:T(8,128)}) %all-reduce.5.cloned.1.call-update) | async-done | bytes 2383888 | tf_op jit(solution)/shard_map/psum | solution.py:462
  528.3 3.2 slice.44
  531.5 1.5 slice_reduce_fusion.1
  533.0 137.3 %shard_map.165 = (f32[12576,768]{1,0:T(8,128)}, f32[12576,128]{1,0:T(8,128)}) custom-call(s32[3]{0:T(128)} %pad_add_fusion.plan_ref, s32[30]{0:T(128)} %compare_select_fusion.6.src_ref, s32[30]{0:T(128)} %compare_select_fusion.5.dst_ref, s32[1,7936]{1,0:T(1,128)} %slice_convert_fusion.lab_ref, ...), custom_call_target="tpu_custom_call", output_to_operand_aliasing={{0}: (7, {}), {1}: (8, {})} | custom-call | flops 99999997952 | bytes 40000000 | tf_op jit(solution)/shard_map/pallas_call | solution.py:328
  670.3 77.5 %shard_map.166 = (f32[12576,768]{1,0:T(8,128)}, f32[12576,128]{1,0:T(8,128)}) custom-call(s32[3]{0:T(128)} %pad_add_fusion.plan_ref, s32[30]{0:T(128)} %compare_select_fusion.6.src_ref, s32[30]{0:T(128)} %compare_select_fusion.5.dst_ref, s32[1,7936]{1,0:T(1,128)} %slice_convert_fusion.lab_ref, ...), custom_call_target="tpu_custom_call", output_to_operand_aliasing={{0}: (7, {}), {1}: (8, {})} | custom-call | flops 49999998976 | bytes 40000000 | tf_op jit(solution)/shard_map/pallas_call | solution.py:328
  747.8 5.1 reduce_sum.112
  (56 shorter events, 6.4 us)
Async XLA Ops:
  8.0 346.9 %all-reduce.3.cloned.1.call-start = ((), (), s32[]{:S(2)}) async-start(), calls=%async_computation | async-start | bytes 15728640 | tf_op jit(solution)/shard_map/psum | solution.py:420
  119.8 2.8 copy-start.3
  120.8 1.8 copy-start.1
  121.3 0.7 copy-start
  201.7 326.6 %all-reduce.5.cloned.1.call-start = ((), (), s32[]{:S(2)}) async-start(), calls=%async_computation.1 | async-start | bytes 4767744 | tf_op jit(solution)/shard_map/psum | solution.py:462
  384.5 3.2 copy-start.10
  384.5 7.8 %copy-start.2 = (f32[4,2560]{1,0:T(4,128)S(1)}, f32[4,2560]{1,0:T(4,128)}, u32[]{:S(2)}) copy-start(f32[4,2560]{1,0:T(4,128)} %copy-done.1) | copy-start | bytes 122884
  384.5 7.8 %copy-start.4 = (pred[4,1,1,2560]{3,0,2,1:T(4,128)(4,1)S(1)}, pred[4,1,1,2560]{3,0,2,1:T(4,128)(4,1)}, u32[]{:S(2)}) copy-start(pred[4,1,1,2560]{3,0,2,1:T(4,128)(4,1)} %copy-done.3) | copy-start | bytes 30724
  384.5 7.8 %copy-start.6 = (f32[4,2560]{1,0:T(4,128)S(1)}, f32[4,2560]{1,0:T(4,128)}, u32[]{:S(2)}) copy-start(f32[4,2560]{1,0:T(4,128)} %get-tuple-element.45) | copy-start | bytes 122884
  384.5 9.2 %copy-start.9 = (f32[4,7936]{1,0:T(4,128)S(1)}, f32[4,7936]{1,0:T(4,128)}, u32[]{:S(2)}) copy-start(f32[4,7936]{1,0:T(4,128)} %constant.175.clone.1) | copy-start | bytes 380932
  384.5 10.1 %copy-start.8 = (f32[4,2560]{1,0:T(4,128)S(1)}, f32[4,2560]{1,0:T(4,128)}, u32[]{:S(2)}) copy-start(f32[4,2560]{1,0:T(4,128)} %get-tuple-element.48) | copy-start | bytes 122884
  384.5 10.8 %copy-start.7 = (f32[4,2560]{1,0:T(4,128)S(1)}, f32[4,2560]{1,0:T(4,128)}, u32[]{:S(2)}) copy-start(f32[4,2560]{1,0:T(4,128)} %get-tuple-element.47) | copy-start | bytes 122884
  384.5 148.4 %all-gather.4.cloned.1.call-start = ((), (), s32[]{:S(2)}) async-start(), calls=%async_computation.2 | async-start | bytes 33423360 | tf_op jit(solution)/shard_map/all_gather | solution.py:379
  396.1 1.7 copy-start.5
Sparse Core Ops, SparseCore 0:
  201.8 153.0 all-reduce.2
  384.7 143.5 all-reduce.4
Sparse Core Ops, SparseCore 1:
  387.7 131.4 all-gather.3
